TPU v7x, 128 devices: a whole 4x4x4 slice. The times are simulated.
128 devices in a mesh: rep: 1, r: 16 (over y, z), s: 8 (over x, core).
Axes of the slice: x: 4, y: 4, z: 4, core: 2. Of those that a mesh axis runs over, the one named last changes fastest.
Arguments:
- x: bfloat16 [128, 2048, 1024], P(('rep', 'r', 's'))
- dy: bfloat16 [128, 2048, 1024], P(('rep', 'r', 's'))
- w_gate: bfloat16 [2, 1024, 3200], P(None, 's')
- w_up: bfloat16 [2, 1024, 3200], P(None, 's')
- w_down: bfloat16 [2, 3200, 1024], P(None, 's')
- m_w_gate: float32 [2, 1024, 3200], P(None, 's')
- m_w_up: float32 [2, 1024, 3200], P(None, 's')
- m_w_down: float32 [2, 3200, 1024], P(None, 's')
- v_w_gate: float32 [2, 1024, 3200], P(None, 's')
- v_w_up: float32 [2, 1024, 3200], P(None, 's')
- v_w_down: float32 [2, 3200, 1024], P(None, 's')
Outputs:
- output 1: bfloat16 [2, 1024, 3200], P('rep', 's')
- output 2: bfloat16 [2, 1024, 3200], P('rep', 's')
- output 3: bfloat16 [2, 3200, 1024], P('rep', 's')
- output 4: float32 [2, 1024, 3200], P('rep', 's')
- output 5: float32 [2, 1024, 3200], P('rep', 's')
- output 6: float32 [2, 3200, 1024], P('rep', 's')
- output 7: float32 [2, 1024, 3200], P('rep', 's')
- output 8: float32 [2, 1024, 3200], P('rep', 's')
- output 9: float32 [2, 3200, 1024], P('rep', 's')
All inputs are finite; a program needn't handle non-finite values.
Results may differ from a plain program's by a relative error of at most 0.022.
Values are sent between devices in bfloat16 or wider.
A program may use at most 1.5 GiB of HBM per device.

v0:
```python
import jax
import jax.numpy as jnp
from jax import lax
from jax.sharding import PartitionSpec as P

NAMES = ("w_gate", "w_up", "w_down")


def matmul(a, w):
    return jnp.dot(a, w, preferred_element_type=jnp.float32).astype(jnp.bfloat16)


def normed(h):
    wide = h.astype(jnp.float32)
    scale = lax.rsqrt(jnp.mean(wide**2, -1, keepdims=True) + 1e-6)
    return (wide * scale).astype(jnp.bfloat16)


def layer(h, w):
    a = normed(h)
    gate = jnp.dot(a, w["w_gate"], preferred_element_type=jnp.float32)
    up = jnp.dot(a, w["w_up"], preferred_element_type=jnp.float32)
    return h + matmul((jax.nn.silu(gate) * up).astype(jnp.bfloat16), w["w_down"])


def adamw(w, m, v, g):
    m = 0.9 * m + 0.1 * g
    v = 0.95 * v + 0.05 * g * g
    step = m * lax.rsqrt(v + 1e-8) + 0.1 * w
    return (w - 0.02 * step).astype(jnp.bfloat16), m, v


def solution(mesh):
    def fetched(weights, number):
        return {name: lax.all_gather(w[number], "s", axis=0, tiled=True) for name, w in zip(NAMES, weights, strict=True)}

    def summed(term):
        return lax.psum(lax.psum_scatter(term, "s", scatter_dimension=0, tiled=True), "r")

    def step(x, dy, *arrays):
        weights, m, v = (arrays[i : i + 3] for i in (0, 3, 6))
        layers = weights[0].shape[0]
        h, kept = x[0], []
        for number in range(layers):
            kept.append(h)
            h = layer(h, fetched(weights, number))
        by_h, mine = dy[0], [None] * layers
        for number in reversed(range(layers)):
            _, back = jax.vjp(lambda w, h: layer(h, w), fetched(weights, number), kept[number])
            by_w, by_h = back(by_h)
            mine[number] = [summed(by_w[name]) for name in NAMES]
        gradients = [jnp.stack([mine[number][i] for number in range(layers)]).astype(jnp.float32) for i in range(3)]
        new = [adamw(w.astype(jnp.float32), m, v, g) for w, m, v, g in zip(weights, m, v, gradients, strict=True)]
        return tuple(one[which] for which in range(3) for one in new)

    states, cut = P(("rep", "r", "s"), None, None), P(None, "s", None)
    return jax.shard_map(
        step,
        mesh=mesh,
        in_specs=(states, states) + (cut,) * 9,
        out_specs=(P("rep", "s", None),) * 9,
        check_vma=False,
    )
```

profile of v0, /device:TPU:0, one launch (start us, length us, event | category | flops | bytes accessed | tf_op | source)
XLA Modules:
  0.0 798.7 jit_solution(6957657372564098524)
XLA Ops:
  7.2 0.0 all-gather.13.cloned.1.call-start
  7.2 2.8 fusion.88
  10.0 0.0 all-gather.13.cloned.1.call-update
  10.0 0.0 all-gather.15.cloned.1.call-start
  10.1 2.7 fusion.87
  12.8 0.0 all-gather.17.cloned.1.call-start
  12.8 1.3 fusion.86
  14.1 0.0 all-gather.17.cloned.1.call-update
  14.2 0.0 all-gather.21.cloned.1.call-start
  14.2 0.5 all-gather.21.cloned.1.call-update
  14.7 0.0 all-gather.23.cloned.1.call-start
  14.8 0.5 all-gather.23.cloned.1.call-update
  15.3 0.0 all-gather.19.cloned.1.call-start
  15.4 0.5 all-gather.19.cloned.1.call-update
  15.9 0.0 reduce-scatter.15.cloned.1.call-start
  15.9 6.5 copy.20
  22.5 3.1 fusion.15
  25.6 6.5 copy.21
  32.1 22.4 %all-gather.13.cloned.1.call-done = bf16[1,1024,3200]{2,1,0:T(8,128)(2,1)} async-done(((bf16[1,128,3200]{2,1,0:T(8,128)(2,1)}), bf16[1,1024,3200]{2,1,0:T(8,128)(2,1)}) %all-gather.13.cloned.1.call-update) | async-done | bytes 6553616 | tf_op jit(solution)/shard_map/all_gather | solution.py:35
  54.5 22.9 %fusion.41 = f32[2048,3200]{1,0:T(8,128)} fusion(bf16[1,1024,3200]{2,1,0:T(8,128)(2,1)} %all-gather.13.cloned.1.call-done, bf16[1,2048,1024]{1,2,0:T(8,128)(2,1)} %copy.20, f32[2048]{0:T(1024)S(1)} %add_rsqrt_fusion), kind=kOutput, calls=%fused_computation.59 | convolution fusion | flops 13428064256 | bytes 36970496 | tf_op jit(solution)/shard_map/dot_general | solution.py:21
  77.3 21.3 %all-gather.15.cloned.1.call-done = bf16[1,1024,3200]{2,1,0:T(8,128)(2,1)} async-done(((bf16[1,128,3200]{2,1,0:T(8,128)(2,1)}), bf16[1,1024,3200]{2,1,0:T(8,128)(2,1)}) %all-gather.15.cloned.1.call-update) | async-done | bytes 6553616 | tf_op jit(solution)/shard_map/all_gather | solution.py:35
  98.6 31.4 %multiply_convert_fusion.1 = (bf16[2048,3200]{1,0:T(8,128)(2,1)}, f32[2048,3200]{1,0:T(8,128)}) fusion(f32[2048,3200]{1,0:T(8,128)} %fusion.41, bf16[1,1024,3200]{2,1,0:T(8,128)(2,1)} %all-gather.15.cloned.1.call-done, bf16[1,2048,1024]{1,2,0:T(8,128)(2,1)} %copy.20, f32[2048]{0:T(1024)S(1)} %add_rsqrt_fusion), kind=kOutput, calls=%fused_computation.17 | convolution fusion | flops 13467385856 | bytes 76292096 | tf_op jit(solution)/shard_map/dot_general | solution.py:22
  130.0 12.8 %all-gather.17.cloned.1.call-done = bf16[1,3200,1024]{2,1,0:T(8,128)(2,1)} async-done(((bf16[1,400,1024]{2,1,0:T(8,128)(2,1)}), bf16[1,3200,1024]{2,1,0:T(8,128)(2,1)}) %all-gather.17.cloned.1.call-update) | async-done | bytes 6553616 | tf_op jit(solution)/shard_map/all_gather | solution.py:35
  142.8 21.9 %fusion.19 = (f32[2048]{0:T(1024)S(1)}, bf16[2048,1024]{0,1:T(8,128)(2,1)}) fusion(bf16[2048,3200]{1,0:T(8,128)(2,1)} %get-tuple-element.30, bf16[1,3200,1024]{2,1,0:T(8,128)(2,1)} %all-gather.17.cloned.1.call-done, bf16[1,2048,1024]{1,2,0:T(8,128)(2,1)} %copy.20), kind=kOutput, calls=%fused_computation.37 | convolution fusion | flops 13432256512 | bytes 28057600 | tf_op jit(solution)/shard_map/dot_general | solution.py:10
  164.7 22.1 %all-gather.21.cloned.1.call-done = bf16[1,3200,1024]{2,1,0:T(8,128)(2,1)} async-done(((bf16[1,400,1024]{2,1,0:T(8,128)(2,1)}), bf16[1,3200,1024]{2,1,0:T(8,128)(2,1)}) %all-gather.21.cloned.1.call-update) | async-done | bytes 6553616 | tf_op jit(solution)/shard_map/all_gather | solution.py:35
  186.8 20.9 %convolution_convert_fusion.1 = bf16[2048,3200]{1,0:T(8,128)(2,1)} fusion(bf16[1,3200,1024]{2,1,0:T(8,128)(2,1)} %all-gather.21.cloned.1.call-done, bf16[1,2048,1024]{2,1,0:T(8,128)(2,1)} %param.12), kind=kOutput, calls=%fused_computation.23 | convolution fusion | flops 13428326400 | bytes 23855104 | tf_op jit(solution)/shard_map/transpose(jvp())/dot_general | solution.py:10
  207.7 23.1 %all-gather.23.cloned.1.call-done = bf16[1,1024,3200]{2,1,0:T(8,128)(2,1)} async-done(((bf16[1,128,3200]{2,1,0:T(8,128)(2,1)}), bf16[1,1024,3200]{2,1,0:T(8,128)(2,1)}) %all-gather.23.cloned.1.call-update) | async-done | bytes 6553616 | tf_op jit(solution)/shard_map/all_gather | solution.py:35
  230.8 22.8 %fusion.28 = f32[2048,3200]{1,0:T(8,128)} fusion(bf16[1,1024,3200]{2,1,0:T(8,128)(2,1)} %all-gather.23.cloned.1.call-done, bf16[2048,1024]{0,1:T(8,128)(2,1)} %get-tuple-element.33, f32[2048]{0:T(1024)S(1)} %fusion.74), kind=kOutput, calls=%fused_computation.46 | convolution fusion | flops 13428064256 | bytes 36970496 | tf_op jit(solution)/shard_map/jvp()/dot_general | solution.py:22
  253.6 21.2 %all-gather.19.cloned.1.call-done = bf16[1,1024,3200]{2,1,0:T(8,128)(2,1)} async-done(((bf16[1,128,3200]{2,1,0:T(8,128)(2,1)}), bf16[1,1024,3200]{2,1,0:T(8,128)(2,1)}) %all-gather.19.cloned.1.call-update) | async-done | bytes 6553616 | tf_op jit(solution)/shard_map/all_gather | solution.py:35
  274.8 38.8 %fusion.2 = (bf16[2048,3200]{1,0:T(8,128)(2,1)}, f32[2048,3200]{1,0:T(8,128)}) fusion(f32[2048,3200]{1,0:T(8,128)} %fusion.28, bf16[2048,3200]{1,0:T(8,128)(2,1)} %convolution_convert_fusion.1, bf16[1,1024,3200]{2,1,0:T(8,128)(2,1)} %all-gather.19.cloned.1.call-done, bf16[2048,1024]{0,1:T(8,128)(2,1)} %get-tuple-element.33, f32[2048]{0:T(1024)S(1)} %fusion.74), kind=kOutput, calls=%fused_computation.8 | convolution fusion | flops 13506707456 | bytes 89399296 | tf_op jit(solution)/shard_map/jvp()/dot_general | solution.py:21
  313.6 22.6 %fusion.12 = bf16[2048,1024]{0,1:T(8,128)(2,1)} fusion(bf16[2048,3200]{1,0:T(8,128)(2,1)} %convolution_convert_fusion.1, bf16[1,1024,3200]{2,1,0:T(8,128)(2,1)} %all-gather.23.cloned.1.call-done, f32[2048,3200]{1,0:T(8,128)} %get-tuple-element.35), kind=kOutput, calls=%fused_computation.21 | convolution fusion | flops 13461094400 | bytes 50069504 | tf_op jit(solution)/shard_map/transpose(jvp())/dot_general | solution.py:22
  336.2 21.8 %fusion.21 = (f32[2048]{0:T(1024)S(1)}, bf16[2048,1024]{0,1:T(8,128)(2,1)}) fusion(bf16[2048,1024]{0,1:T(8,128)(2,1)S(1)} %copy-done.6, bf16[2048,1024]{0,1:T(8,128)(2,1)} %fusion.12, bf16[2048,3200]{1,0:T(8,128)(2,1)} %get-tuple-element.34, bf16[1,1024,3200]{2,1,0:T(8,128)(2,1)} %all-gather.19.cloned.1.call-done), kind=kOutput, calls=%fused_computation.39 | convolution fusion | flops 13432256512 | bytes 32251904 | tf_op jit(solution)/shard_map/transpose(jvp())/dot_general | solution.py:21
  358.0 4.9 fusion.44
  362.9 2.1 copy-done.7
  365.0 19.5 %convolution_convert_fusion.2 = bf16[3200,1024]{1,0:T(8,128)(2,1)} fusion(bf16[2048,3200]{1,0:T(8,128)(2,1)} %get-tuple-element.30, bf16[2048,1024]{0,1:T(8,128)(2,1)S(1)} %fusion.44), kind=kOutput, calls=%fused_computation.44 | convolution fusion | flops 13425049600 | bytes 23855104 | tf_op jit(solution)/shard_map/transpose(jvp())/dot_general | solution.py:10
  384.5 0.0 reduce-scatter.17.cloned.1.call-start
  384.6 26.0 %fusion.25 = bf16[3200,1024]{1,0:T(8,128)(2,1)} fusion(f32[2048,3200]{1,0:T(8,128)} %fusion.28, bf16[1,2048,1024]{2,1,0:T(8,128)(2,1)} %param.12, f32[2048,3200]{1,0:T(8,128)} %get-tuple-element.35), kind=kOutput, calls=%fused_computation.41 | convolution fusion | flops 13464371200 | bytes 63176704 | tf_op jit(solution)/shard_map/transpose(jvp())/dot_general | solution.py:10
  410.6 0.0 reduce-scatter.17.cloned.1.call-update
  410.6 0.0 reduce-scatter.11.cloned.1.call-start
  410.7 21.4 %convolution_convert_fusion = bf16[2048,3200]{1,0:T(8,128)(2,1)} fusion(bf16[2048,1024]{0,1:T(8,128)(2,1)} %copy-done.7, bf16[1,3200,1024]{2,1,0:T(8,128)(2,1)} %all-gather.17.cloned.1.call-done), kind=kOutput, calls=%fused_computation.22 | convolution fusion | flops 13428326400 | bytes 23855104 | tf_op jit(solution)/shard_map/transpose(jvp())/dot_general | solution.py:10
  432.1 24.3 %fusion.27 = bf16[1024,3200]{1,0:T(8,128)(2,1)} fusion(bf16[2048,3200]{1,0:T(8,128)(2,1)} %convolution_convert_fusion, f32[2048,3200]{1,0:T(8,128)} %fusion.41, bf16[1,2048,1024]{1,2,0:T(8,128)(2,1)S(1)} %copy-done.1, f32[2048]{0:T(1024)S(1)} %copy-done.19), kind=kOutput, calls=%fused_computation.43 | convolution fusion | flops 13470662656 | bytes 50077696 | tf_op jit(solution)/shard_map/transpose(jvp())/dot_general | solution.py:22
  456.5 0.0 reduce-scatter.13.cloned.1.call-start
  456.5 0.6 copy-done.15
  457.2 25.4 %fusion.26 = bf16[1024,3200]{1,0:T(8,128)(2,1)} fusion(bf16[2048,3200]{1,0:T(8,128)(2,1)} %convolution_convert_fusion.1, bf16[2048,1024]{0,1:T(8,128)(2,1)} %get-tuple-element.33, f32[2048]{0:T(1024)S(1)} %copy-done.15, f32[2048,3200]{1,0:T(8,128)} %get-tuple-element.35), kind=kOutput, calls=%fused_computation.42 | convolution fusion | flops 13470662656 | bytes 50077696 | tf_op jit(solution)/shard_map/transpose(jvp())/dot_general | solution.py:22
  482.6 0.0 reduce-scatter.7.cloned.1.call-start
  482.6 32.6 %fusion.22 = bf16[1024,3200]{1,0:T(8,128)(2,1)} fusion(f32[2048,3200]{1,0:T(8,128)} %fusion.41, f32[2048,3200]{1,0:T(8,128)} %get-tuple-element.31, bf16[2048,3200]{1,0:T(8,128)(2,1)} %convolution_convert_fusion, bf16[1,2048,1024]{1,2,0:T(8,128)(2,1)} %copy.20, f32[2048]{0:T(1024)S(1)} %copy-done.19), kind=kOutput, calls=%fused_computation.40 | convolution fusion | flops 13503430656 | bytes 76292096 | tf_op jit(solution)/shard_map/transpose(jvp())/dot_general | solution.py:21
  515.2 0.0 reduce-scatter.9.cloned.1.call-start
  515.3 21.0 %convolution_convert_fusion.3 = bf16[1024,3200]{1,0:T(8,128)(2,1)} fusion(bf16[2048,3200]{1,0:T(8,128)(2,1)} %get-tuple-element.34, bf16[2048,1024]{0,1:T(8,128)(2,1)} %get-tuple-element.33, f32[2048]{0:T(1024)S(1)} %copy-done.15), kind=kOutput, calls=%fused_computation.45 | convolution fusion | flops 13428064256 | bytes 23863296 | tf_op jit(solution)/shard_map/transpose(jvp())/dot_general | solution.py:21
  536.3 0.0 all-reduce.3.cloned.1.call-start
  536.4 0.0 reduce-scatter.15.cloned.1.call-done
  536.4 0.0 reduce-scatter.17.cloned.1.call-done
  536.4 0.0 reduce-scatter.11.cloned.1.call-done
  536.4 29.7 %reduce-scatter.13.cloned.1.call-done = bf16[128,3200]{1,0:T(8,128)(2,1)} async-done(((bf16[1024,3200]{1,0:T(8,128)(2,1)}), bf16[128,3200]{1,0:T(8,128)(2,1)}) %reduce-scatter.13.cloned.1.call-update) | async-done | bytes 819216 | tf_op jit(solution)/shard_map/reduce_scatter | solution.py:38
  566.2 45.9 %reduce-scatter.7.cloned.1.call-done = bf16[128,3200]{1,0:T(8,128)(2,1)} async-done(((bf16[1024,3200]{1,0:T(8,128)(2,1)}), bf16[128,3200]{1,0:T(8,128)(2,1)}) %reduce-scatter.7.cloned.1.call-update) | async-done | bytes 819216 | tf_op jit(solution)/shard_map/reduce_scatter | solution.py:38
  612.1 45.8 %reduce-scatter.9.cloned.1.call-done = bf16[128,3200]{1,0:T(8,128)(2,1)} async-done(((bf16[1024,3200]{1,0:T(8,128)(2,1)}), bf16[128,3200]{1,0:T(8,128)(2,1)}) %reduce-scatter.9.cloned.1.call-update) | async-done | bytes 819216 | tf_op jit(solution)/shard_map/reduce_scatter | solution.py:38
  657.9 114.0 %all-reduce.3.cloned.1.call-done = (bf16[1,128,3200]{2,1,0:T(8,128)(2,1)}, bf16[1,128,3200]{2,1,0:T(8,128)(2,1)}, bf16[1,128,3200]{2,1,0:T(8,128)(2,1)}, bf16[1,...) async-done(((bf16[1,128,3200]{2,1,0:T(8,128)(2,1)}, bf16[1,128,3200]{2,1,0:T(8,128)(2,1)}, bf16[1,128,3200]{2,1,0:T(8,128)(2,1)}, ...) | async-done | bytes 4915216 | tf_op jit(solution)/shard_map/psum | solution.py:38
  771.9 7.4 fusion.61
  779.3 0.3 copy-done.8
  779.6 1.4 copy-done.9
  781.0 0.9 copy-done.10
  782.0 0.9 copy-done.11
  782.9 0.1 copy-done.12
  783.0 0.2 copy-done.13
  783.3 8.7 %fusion.53 = (bf16[2,128,3200]{2,1,0:T(8,128)(2,1)}, f32[2,128,3200]{2,1,0:T(8,128)}, f32[2,128,3200]{2,1,0:T(8,128)}, bf16[2,128,3200]{2,1,0:T(8,128)(2,1)}, f3...) fusion(bf16[2,128,3200]{2,1,0:T(8,128)(2,1)S(1)} %copy-done.4, bf16[1,128,3200]{2,1,0:T(8,128)(2,1)S(1)} %copy-done.12, ...), kind=kLoop, calls=%fused_computation.80 | loop fusion | flops 31129600 | bytes 36044800 | tf_op jit(solution)/shard_map/convert_element_type | solution.py:30
  (42 shorter events, 0.2 us)
Async XLA Ops:
  7.2 5.7 copy-start.2
  7.2 47.3 %all-gather.13.cloned.1.call-start = ((), (), s32[]{:S(2)}) async-start(), calls=%async_computation.12 | async-start | bytes 7372800 | tf_op jit(solution)/shard_map/all_gather | solution.py:35
  10.0 88.6 %all-gather.15.cloned.1.call-start = ((), (), s32[]{:S(2)}) async-start(), calls=%async_computation.13 | async-start | bytes 7372800 | tf_op jit(solution)/shard_map/all_gather | solution.py:35
  12.8 130.0 %all-gather.17.cloned.1.call-start = ((), (), s32[]{:S(2)}) async-start(), calls=%async_computation.14 | async-start | bytes 7372800 | tf_op jit(solution)/shard_map/all_gather | solution.py:35
  14.2 172.6 %all-gather.21.cloned.1.call-start = ((), (), s32[]{:S(2)}) async-start(), calls=%async_computation.16 | async-start | bytes 7372800 | tf_op jit(solution)/shard_map/all_gather | solution.py:35
  14.7 216.1 %all-gather.23.cloned.1.call-start = ((), (), s32[]{:S(2)}) async-start(), calls=%async_computation.17 | async-start | bytes 7372800 | tf_op jit(solution)/shard_map/all_gather | solution.py:35
  15.3 259.5 %all-gather.19.cloned.1.call-start = ((), (), s32[]{:S(2)}) async-start(), calls=%async_computation.15 | async-start | bytes 7372800 | tf_op jit(solution)/shard_map/all_gather | solution.py:35
  15.9 520.5 %reduce-scatter.15.cloned.1.call-start = ((), (), s32[]{:S(2)}) async-start(), calls=%async_computation.10 | async-start | bytes 7372800 | tf_op jit(solution)/shard_map/reduce_scatter | solution.py:38
  25.6 73.1 %copy-start.18 = (f32[2048]{0:T(1024)}, f32[2048]{0:T(1024)S(1)}, u32[]{:S(2)}) copy-start(f32[2048]{0:T(1024)S(1)} %add_rsqrt_fusion) | copy-start | bytes 24580
  164.7 43.0 %copy-start.16 = (f32[2048]{0:T(1024)}, f32[2048]{0:T(1024)S(1)}, u32[]{:S(2)}) copy-start(f32[2048]{0:T(1024)S(1)} %get-tuple-element.32) | copy-start | bytes 24580
  164.7 193.3 %copy-start.14 = (f32[2048]{0:T(1024)}, f32[2048]{0:T(1024)S(1)}, u32[]{:S(2)}) copy-start(f32[2048]{0:T(1024)S(1)} %fusion.74) | copy-start | bytes 24580
  313.6 22.6 %copy-start.6 = (bf16[2048,1024]{0,1:T(8,128)(2,1)S(1)}, bf16[2048,1024]{0,1:T(8,128)(2,1)}, u32[]{:S(2)}) copy-start(bf16[2048,1024]{0,1:T(8,128)(2,1)} %get-tuple-element.33) | copy-start | bytes 12582916
  336.2 21.8 %copy-start.17 = (f32[2048]{0:T(1024)S(1)}, f32[2048]{0:T(1024)}, u32[]{:S(2)}) copy-start(f32[2048]{0:T(1024)} %copy-done.16) | copy-start | bytes 24580
  336.2 21.8 %copy-start = (bf16[1,2048,1024]{1,2,0:T(8,128)(2,1)S(1)}, bf16[1,2048,1024]{1,2,0:T(8,128)(2,1)}, u32[]{:S(2)}) copy-start(bf16[1,2048,1024]{1,2,0:T(8,128)(2,1)} %copy.21) | copy-start | bytes 12582916
  362.9 2.1 copy-start.7
  384.5 151.9 %reduce-scatter.17.cloned.1.call-start = ((), (), s32[]{:S(2)}) async-start(), calls=%async_computation.11 | async-start | bytes 7372800 | tf_op jit(solution)/shard_map/reduce_scatter | solution.py:38
  410.6 21.5 %copy-start.19 = (f32[2048]{0:T(1024)S(1)}, f32[2048]{0:T(1024)}, u32[]{:S(2)}) copy-start(f32[2048]{0:T(1024)} %copy-done.18) | copy-start | bytes 24580
  410.6 125.8 %reduce-scatter.11.cloned.1.call-start = ((), (), s32[]{:S(2)}) async-start(), calls=%async_computation.8 | async-start | bytes 7372800 | tf_op jit(solution)/shard_map/reduce_scatter | solution.py:38
  410.7 21.5 %copy-start.1 = (bf16[1,2048,1024]{1,2,0:T(8,128)(2,1)S(1)}, bf16[1,2048,1024]{1,2,0:T(8,128)(2,1)}, u32[]{:S(2)}) copy-start(bf16[1,2048,1024]{1,2,0:T(8,128)(2,1)} %copy.20) | copy-start | bytes 12582916
  456.5 0.7 copy-start.15
  456.5 109.7 %reduce-scatter.13.cloned.1.call-start = ((), (), s32[]{:S(2)}) async-start(), calls=%async_computation.9 | async-start | bytes 7372800 | tf_op jit(solution)/shard_map/reduce_scatter | solution.py:38
  482.6 129.5 %reduce-scatter.7.cloned.1.call-start = ((), (), s32[]{:S(2)}) async-start(), calls=%async_computation.6 | async-start | bytes 7372800 | tf_op jit(solution)/shard_map/reduce_scatter | solution.py:38
  515.2 142.6 %reduce-scatter.9.cloned.1.call-start = ((), (), s32[]{:S(2)}) async-start(), calls=%async_computation.7 | async-start | bytes 7372800 | tf_op jit(solution)/shard_map/reduce_scatter | solution.py:38
  536.3 235.6 %copy-start.3 = (bf16[2,400,1024]{2,1,0:T(8,128)(2,1)S(1)}, bf16[2,400,1024]{2,1,0:T(8,128)(2,1)}, u32[]{:S(2)}) copy-start(bf16[2,400,1024]{2,1,0:T(8,128)(2,1)} %param.15) | copy-start | bytes 4915204
  536.3 235.5 %all-reduce.3.cloned.1.call-start = ((), (), s32[]{:S(2)}) async-start(), calls=%async_computation.18 | async-start | bytes 9830400 | tf_op jit(solution)/shard_map/psum | solution.py:38
  771.9 7.4 copy-start.4
  771.9 7.4 copy-start.5
  771.9 7.7 copy-start.8
  771.9 9.2 %copy-start.9 = (f32[2,128,3200]{2,1,0:T(8,128)S(1)}, f32[2,128,3200]{2,1,0:T(8,128)}, u32[]{:S(2)}) copy-start(f32[2,128,3200]{2,1,0:T(8,128)} %param.16) | copy-start | bytes 9830404
  771.9 10.1 %copy-start.10 = (f32[2,128,3200]{2,1,0:T(8,128)S(1)}, f32[2,128,3200]{2,1,0:T(8,128)}, u32[]{:S(2)}) copy-start(f32[2,128,3200]{2,1,0:T(8,128)} %param.20) | copy-start | bytes 9830404
  771.9 11.0 %copy-start.11 = (f32[2,128,3200]{2,1,0:T(8,128)S(1)}, f32[2,128,3200]{2,1,0:T(8,128)}, u32[]{:S(2)}) copy-start(f32[2,128,3200]{2,1,0:T(8,128)} %param.17) | copy-start | bytes 9830404
  771.9 11.1 %copy-start.12 = (bf16[1,128,3200]{2,1,0:T(8,128)(2,1)S(1)}, bf16[1,128,3200]{2,1,0:T(8,128)(2,1)}, u32[]{:S(2)}) copy-start(bf16[1,128,3200]{2,1,0:T(8,128)(2,1)} %get-tuple-element.9) | copy-start | bytes 2457604
  771.9 11.4 %copy-start.13 = (bf16[1,128,3200]{2,1,0:T(8,128)(2,1)S(1)}, bf16[1,128,3200]{2,1,0:T(8,128)(2,1)}, u32[]{:S(2)}) copy-start(bf16[1,128,3200]{2,1,0:T(8,128)(2,1)} %get-tuple-element.10) | copy-start | bytes 2457604
Sparse Core Ops, SparseCore 0:
  10.3 44.1 all-gather.12
  56.7 41.8 all-gather.14
  100.9 41.8 all-gather.16
  144.9 41.8 all-gather.20
  188.9 41.8 all-gather.22
  232.9 41.8 all-gather.18
  384.7 43.9 reduce-scatter.14
  431.0 43.4 reduce-scatter.16
  476.9 43.4 reduce-scatter.10
  522.7 43.4 reduce-scatter.12
  568.6 43.4 reduce-scatter.6
  614.4 43.4 reduce-scatter.8
  662.1 109.7 all-reduce.2
where the time goes:
time: 807 us; the launch traced here: 799 us
  matrix products  373 us (46%)
  waiting for transfers between devices  360 us (45%)
  local copies, waits for them, and re-layouts  26.5 us (3%)
  other arithmetic  24 us (3%)
  between operations  14.3 us (2%)
    dot_general x5, matrix products, layer(): gate = jnp.dot(a, w['w_gate'], preferred_element_type=jnp.float32)  137 us
    dot_general x5, matrix products, layer(): up = jnp.dot(a, w['w_up'], preferred_element_type=jnp.float32)  126 us
    all_gather x6, waiting for transfers between devices, fetched(): lax.all_gather(w[number], 's', axis=0, tiled=True)  123 us
    reduce_scatter x6, waiting for transfers between devices, summed(): lax.psum_scatter(term, 's', scatter_dimension=0, tiled=True)  121 us
    psum x1, waiting for transfers between devices, summed(): lax.psum(lax.psum_scatter(term, 's', scatter_dimension=0, tiled=True), 'r')  114 us
    dot_general x5, matrix products, matmul(): jnp.dot(a, w, preferred_element_type=jnp.float32).astype(jnp.bfloat16)  110 us
    unnamed x42, local copies, waits for them, and re-layouts  19.8 us
  transfers between devices with their start and end apart: 13, of which 10 were waited for; matrix products, arithmetic and copies ran while one was open for 36% of the time, Pallas kernels for 0%

commit v1 on v0

v1 whole, which is shorter than its diff:
```python
import functools

import jax
import jax.numpy as jnp
from jax import lax
from jax.experimental import pallas as pl
from jax.experimental.pallas import tpu as pltpu
from jax.sharding import PartitionSpec as P

BF, F32 = jnp.bfloat16, jnp.float32
MESH = pl.DeviceIdType.MESH
VMEM_LIMIT = 66_000_000
T, D, FF = 2048, 1024, 3200
TM = 512
CHUNKS = tuple((512 * j, 512) for j in range(6)) + ((3072, 128),)
GROUPS = ((0, 1024), (1024, 2176))
ANY = pl.BlockSpec(memory_space=pl.ANY)


def dot(a, b):
    return jnp.dot(a, b, preferred_element_type=F32)


def dot_bt(a, b):
    return lax.dot_general(a, b, (((1,), (1,)), ((), ())), preferred_element_type=F32)


def dot_at(a, b):
    return lax.dot_general(a, b, (((0,), (0,)), ((), ())), preferred_element_type=F32)


def normed(h):
    wide = h.astype(F32)
    scale = lax.rsqrt(jnp.mean(wide * wide, -1, keepdims=True) + 1e-6)
    return (wide * scale).astype(BF)


def cost(matmuls, nbytes):
    return pl.CostEstimate(flops=matmuls * 2 * T * D * FF, bytes_accessed=nbytes, transcendentals=0)


def forward_kernel(
    x_hbm, g_hbm, u_hbm, d_hbm,
    G, U, Dn, hid_hbm, a_hbm, h_hbm,
    x, stage_g, stage_u, stage_d, wg, wu, wd, hid, a_nat, a_t, hid_t,
    s1, r1, s2, r2, s3, r3, stage_sem, own_sem, x_sem, w_sem, hid_sem, a_sem, h_sem,
):
    r, s = lax.axis_index("r"), lax.axis_index("s")
    y, z = r // 4, r % 4
    cx, core = s // 2, s % 2

    def at_x(k):
        return {"r": r, "s": 2 * ((cx + k) % 4) + core}

    def at_y(k):
        return {"r": ((y + k) % 4) * 4 + z, "s": s}

    def at_z(k):
        return {"r": y * 4 + (z + k) % 4, "s": s}

    partner = {"r": r, "s": s + 1 - 2 * core}

    barrier = pltpu.get_barrier_semaphore()
    for to in [at(k) for at in (at_x, at_y, at_z) for k in (1, 2, 3)] + [partner]:
        pl.semaphore_signal(barrier, inc=1, device_id=to, device_id_type=MESH)
    pl.semaphore_wait(barrier, 10)

    mats = [m for l in range(2) for m in ((g_hbm, l, G, stage_g, 128), (u_hbm, l, U, stage_u, 128), (d_hbm, l, Dn, stage_d, 400))]

    def piece(rows, half, j):
        if rows == 128:
            return pl.ds(pl.multiple_of(half * 64 + j * 16, 16), 16), slice(None)
        return slice(None), pl.ds(pl.multiple_of(half * 512 + j * 128, 128), 128)

    def block(whole, l, b, rows, half=None, j=None):
        if half is None:
            return whole.at[l, b]
        p = piece(rows, half, j)
        return whole.at[l, b, p[0], p[1]]

    def c1(i, half, k):
        shard, l, whole, _, rows = mats[i]
        j = (y, z)[half]
        p = piece(rows, half, j)
        return pltpu.make_async_remote_copy(
            src_ref=shard.at[l, p[0], p[1]], dst_ref=block(whole, l, s, rows, half, j),
            send_sem=s1.at[i, half, k - 1], recv_sem=r1.at[i, half, k - 1], device_id=at_x(k), device_id_type=MESH)

    def c2(i, half, k, q):
        _, l, whole, _, rows = mats[i]
        b = 2 * ((cx + 4 - k) % 4) + core
        ref = block(whole, l, b, rows, half, (y, z)[half])
        return pltpu.make_async_remote_copy(
            src_ref=ref, dst_ref=ref, send_sem=s2.at[i, half, k - 1, q - 1], recv_sem=r2.at[i, half, k - 1, q - 1],
            device_id=(at_y, at_z)[half](q), device_id_type=MESH)

    def c3(i, k):
        shard, l, whole, _, rows = mats[i]
        b = 2 * ((cx + 4 - k) % 4) + core
        src = shard.at[l] if k == 0 else whole.at[l, b]
        return pltpu.make_async_remote_copy(
            src_ref=src, dst_ref=whole.at[l, b], send_sem=s3.at[i, k], recv_sem=r3.at[i, k], device_id=partner, device_id_type=MESH)

    def stage_in(i):
        shard, l, _, stage, _ = mats[i]
        return pltpu.make_async_copy(shard.at[l], stage.at[l], stage_sem.at[i])

    def stage_out(i):
        _, l, whole, stage, _ = mats[i]
        return pltpu.make_async_copy(stage.at[l], whole.at[l, s], own_sem.at[i])

    near_first = (1, 3, 2)

    def p1(i):
        for k in near_first:
            for half in range(2):
                c1(i, half, k).start()
        c3(i, 0).start()

    def p2(i):
        for k in near_first:
            for half in range(2):
                c1(i, half, k).wait_recv()
                for q in near_first:
                    c2(i, half, k, q).start()

    def p3(i):
        for k in near_first:
            for half in range(2):
                for q in near_first:
                    c2(i, half, k, q).wait_recv()
            c3(i, k).start()

    def arrived(i):
        for k in range(4):
            c3(i, k).wait_recv()

    loads = {0: wg, 1: wu, 2: wd}

    def load(i, b):
        _, l, whole, _, rows = mats[i]
        return pltpu.make_async_copy(whole.at[l, b], loads[i].at[pl.ds(b * rows, rows)], w_sem.at[i, b])

    def load_start(i):
        arrived(i)
        stage_out(i).wait()
        for b in range(8):
            load(i, b).start()

    def load_wait(i):
        for b in range(8):
            load(i, b).wait()

    for i in range(6):
        stage_in(i).start()
    for i in range(6):
        p1(i)
    x_copy = pltpu.make_async_copy(x_hbm, x, x_sem)
    x_copy.start()
    for i in range(6):
        stage_in(i).wait()
        stage_out(i).start()
    p2(0)
    p2(1)
    p3(0)
    p2(2)
    p2(3)
    load_start(0)
    p3(1)
    p2(4)
    load_start(1)
    x_copy.wait()
    load_wait(0)
    load_wait(1)

    def rows_of(m):
        return pl.ds(pl.multiple_of(m * TM, TM), TM)

    def hid_copy(m):
        return pltpu.make_async_copy(hid_t, hid_hbm.at[:, rows_of(m)], hid_sem.at[m])

    def a_copy(m):
        return pltpu.make_async_copy(a_t, a_hbm.at[:, rows_of(m)], a_sem.at[m])

    def h_copy(m):
        return pltpu.make_async_copy(x.at[rows_of(m)], h_hbm.at[rows_of(m)], h_sem.at[m])

    def up_step(m, carry):
        a = normed(x[rows_of(m), :])
        a_nat[...] = a

        @pl.when(m > 0)
        def _():
            a_copy(m - 1).wait()
            hid_copy(m - 1).wait()

        a_t[...] = a.T
        for start, size in CHUNKS:
            columns = pl.ds(start, size)
            gate, up = dot(a_nat[...], wg[:, columns]), dot(a_nat[...], wu[:, columns])
            one = (jax.nn.silu(gate) * up).astype(BF)
            hid[rows_of(m), columns] = one
            hid_t[columns, :] = one.T
        hid_copy(m).start()
        a_copy(m).start()

        @pl.when(m == 0)
        def _():
            p2(5)
            p3(2)

        @pl.when(m == 1)
        def _():
            p3(3)
            load_start(2)

        @pl.when(m == 2)
        def _():
            p3(4)

        return carry

    def down_step(m, carry):
        out = dot(hid[rows_of(m), :], wd[...]).astype(BF)
        x[rows_of(m), :] = (x[rows_of(m), :].astype(F32) + out.astype(F32)).astype(BF)
        h_copy(m).start()

        @pl.when(m == 1)
        def _():
            p3(5)

        return carry

    lax.fori_loop(0, 4, up_step, 0)
    load_wait(2)
    lax.fori_loop(0, 4, down_step, 0)

    for i in range(6):
        if i > 2:
            arrived(i)
            stage_out(i).wait()
        for k in (1, 2, 3):
            for half in range(2):
                c1(i, half, k).wait_send()
                for q in (1, 2, 3):
                    c2(i, half, k, q).wait_send()
        for k in range(4):
            c3(i, k).wait_send()
    hid_copy(3).wait()
    a_copy(3).wait()
    for m in range(4):
        h_copy(m).wait()


def forward(x, g, u, d):
    dma = pltpu.SemaphoreType.DMA
    return pl.pallas_call(
        forward_kernel,
        out_shape=(
            jax.ShapeDtypeStruct((2, 8, 128, FF), BF),
            jax.ShapeDtypeStruct((2, 8, 128, FF), BF),
            jax.ShapeDtypeStruct((2, 8, 400, D), BF),
            jax.ShapeDtypeStruct((FF, T), BF),
            jax.ShapeDtypeStruct((D, T), BF),
            jax.ShapeDtypeStruct((T, D), BF),
        ),
        in_specs=[ANY] * 4,
        out_specs=(ANY,) * 6,
        scratch_shapes=[
            pltpu.VMEM((T, D), BF),
            pltpu.VMEM((2, 128, FF), BF),
            pltpu.VMEM((2, 128, FF), BF),
            pltpu.VMEM((2, 400, D), BF),
            pltpu.VMEM((D, FF), BF),
            pltpu.VMEM((D, FF), BF),
            pltpu.VMEM((FF, D), BF),
            pltpu.VMEM((T, FF), BF),
            pltpu.VMEM((TM, D), BF),
            pltpu.VMEM((D, TM), BF),
            pltpu.VMEM((FF, TM), BF),
            dma((6, 2, 3)), dma((6, 2, 3)), dma((6, 2, 3, 3)), dma((6, 2, 3, 3)), dma((6, 4)), dma((6, 4)),
            dma((6,)), dma((6,)), dma, dma((3, 8)), dma((4,)), dma((4,)), dma((4,)),
        ],
        compiler_params=pltpu.CompilerParams(collective_id=0, has_side_effects=True, vmem_limit_bytes=VMEM_LIMIT),
        cost_estimate=cost(3, 60_000_000),
        name="forward",
    )(x, g, u, d)


def hidden_kernel(number, want_hid, h, by_y, G, U, Dn, *rest):
    outs, (a_nat, wg, wu, wd, sems) = rest[:-5], rest[-5:]
    hid_ref, a_ref = outs[:2] if want_hid else (None, None)
    dg_ref, du_ref = outs[-2:]
    m = pl.program_id(0)

    def copies(j):
        part = pl.ds(*GROUPS[j])
        return (
            pltpu.make_async_copy(G.at[number, :, part], wg.at[:, part], sems.at[0, j]),
            pltpu.make_async_copy(U.at[number, :, part], wu.at[:, part], sems.at[1, j]),
            pltpu.make_async_copy(Dn.at[number, part, :], wd.at[part, :], sems.at[2, j]),
        )

    @pl.when(m == 0)
    def _():
        for j in range(len(GROUPS)):
            for copy in copies(j):
                copy.start()

    a = normed(h[...])
    a_nat[...] = a
    if want_hid:
        a_ref[...] = a.T
    for j, (first, count) in enumerate(GROUPS):

        @pl.when(m == 0)
        def _():
            for copy in copies(j):
                copy.wait()

        for start, size in CHUNKS:
            if not first <= start < first + count:
                continue
            part = pl.ds(start, size)
            gate, up = dot(a_nat[...], wg[:, part]), dot(a_nat[...], wu[:, part])
            by_hid = dot_bt(by_y[...], wd[part, :]).astype(BF).astype(F32)
            sig = jax.nn.sigmoid(gate)
            act = gate * sig
            if want_hid:
                hid_ref[part, :] = (act * up).astype(BF).T
            du_ref[:, part] = (by_hid * act).astype(BF)
            dg_ref[:, part] = (by_hid * up * (sig + act * (1.0 - sig))).astype(BF)


def hidden(number, want_hid, h, by_y, G, U, Dn):
    tile = pl.BlockSpec((TM, D), lambda m: (m, 0))
    wide = pl.BlockSpec((TM, FF), lambda m: (m, 0))
    wide_shape = jax.ShapeDtypeStruct((T, FF), BF)
    extra_specs = (pl.BlockSpec((FF, TM), lambda m: (0, m)), pl.BlockSpec((D, TM), lambda m: (0, m))) if want_hid else ()
    extra_shapes = (jax.ShapeDtypeStruct((FF, T), BF), jax.ShapeDtypeStruct((D, T), BF)) if want_hid else ()
    return pl.pallas_call(
        functools.partial(hidden_kernel, number, want_hid),
        grid=(T // TM,),
        out_shape=extra_shapes + (wide_shape, wide_shape),
        in_specs=[tile, tile, ANY, ANY, ANY],
        out_specs=extra_specs + (wide, wide),
        scratch_shapes=[
            pltpu.VMEM((TM, D), BF),
            pltpu.VMEM((D, FF), BF),
            pltpu.VMEM((D, FF), BF),
            pltpu.VMEM((FF, D), BF),
            pltpu.SemaphoreType.DMA((3, len(GROUPS))),
        ],
        compiler_params=pltpu.CompilerParams(vmem_limit_bytes=VMEM_LIMIT, dimension_semantics=("arbitrary",)),
        cost_estimate=cost(3, 70_000_000),
        name=f"hidden_{number}",
    )(h, by_y, G.reshape(2, D, FF), U.reshape(2, D, FF), Dn.reshape(2, FF, D))


def input_kernel(number, h, by_y, dg, du, G, U, out, wg, wu, sems):
    m = pl.program_id(0)
    copies = [pltpu.make_async_copy(W.at[number], w, sems.at[i]) for i, (W, w) in enumerate(((G, wg), (U, wu)))]

    @pl.when(m == 0)
    def _():
        copies[0].start()
        copies[1].start()
        copies[0].wait()

    by_a = dot_bt(dg[...], wg[...]).astype(BF).astype(F32)

    @pl.when(m == 0)
    def _():
        copies[1].wait()

    by_a = (by_a + dot_bt(du[...], wu[...]).astype(BF).astype(F32)).astype(BF).astype(F32)
    wide = h[...].astype(F32)
    scale = lax.rsqrt(jnp.mean(wide * wide, -1, keepdims=True) + 1e-6)
    along = jnp.mean(by_a * wide, -1, keepdims=True)
    by_h = (by_a * scale - wide * (scale * scale * scale * along)).astype(BF)
    out[...] = (by_y[...].astype(F32) + by_h.astype(F32)).astype(BF)


def input_gradient(number, h, by_y, dg, du, G, U):
    tile = pl.BlockSpec((TM, D), lambda m: (m, 0))
    wide = pl.BlockSpec((TM, FF), lambda m: (m, 0))
    return pl.pallas_call(
        functools.partial(input_kernel, number),
        grid=(T // TM,),
        out_shape=jax.ShapeDtypeStruct((T, D), BF),
        in_specs=[tile, tile, wide, wide, ANY, ANY],
        out_specs=tile,
        scratch_shapes=[pltpu.VMEM((D, FF), BF), pltpu.VMEM((D, FF), BF), pltpu.SemaphoreType.DMA((2,))],
        compiler_params=pltpu.CompilerParams(vmem_limit_bytes=VMEM_LIMIT, dimension_semantics=("arbitrary",)),
        cost_estimate=cost(2, 50_000_000),
        name=f"input_{number}",
    )(h, by_y, dg, du, G.reshape(2, D, FF), U.reshape(2, D, FF))


UNITS = (
    ((64, 256), "yxz", "zy"),
    ((48, 256), "zxy", "yz"),
    ((16, 512), "xyz", "zy"),
    ((16, 512), "xzy", "yz"),
    ((16, 512), "yxz", "zy"),
    ((16, 512), "xzy", "yz"),
    ((16, 512), "xyz", "zy"),
    ((16, 512), "zxy", "yz"),
    ((16, 128), "xyz", "yz"),
)
NEAR_FIRST = (1, 3, 2)
KINDS = ((0, 1), (1, 1), (2, 6), (8, 1))


def gradients_kernel(
    aT, hidT, dg, du, by_y, g_out, u_out, d_out,
    a, rhs, rhs_tail, hid, send_d, send_e, send_u, send_t,
    *rest,
):
    bufs, (pair_s, pair_r, s, r, a_sem, rhs_sem, tail_sem, hid_sem, y_sem, out_sem) = rest[:32], rest[32:]
    ri, si = lax.axis_index("r"), lax.axis_index("s")
    core = si % 2
    me = {"x": si // 2, "y": ri // 4, "z": ri % 4}

    def peer(axis, k):
        if axis == "x":
            return {"r": ri, "s": 2 * ((me["x"] + k) % 4) + core}
        if axis == "y":
            return {"r": ((me["y"] + k) % 4) * 4 + me["z"], "s": si}
        return {"r": me["y"] * 4 + (me["z"] + k) % 4, "s": si}

    partner = {"r": ri, "s": si + 1 - 2 * core}
    barrier = pltpu.get_barrier_semaphore()
    for to in [peer(axis, k) for axis in "xyz" for k in (1, 2, 3)] + [partner]:
        pl.semaphore_signal(barrier, inc=1, device_id=to, device_id_type=MESH)
    pl.semaphore_wait(barrier, 10)

    def buffers(unit):
        for kind, (first, count) in enumerate(KINDS):
            if first <= unit < first + count:
                return [ref.at[unit - first] for ref in bufs[8 * kind : 8 * kind + 8]]

    def others(unit, stage):
        order = UNITS[unit][1]
        return [axis for axis in "xyz" if axis in order[stage:]]

    def cut(unit, stage, index):
        return tuple(index if axis == UNITS[unit][1][stage] else slice(None) for axis in others(unit, stage))

    def copies(unit, stage):
        P, R1, Q1, F1, R2, Q2, F2, RA = buffers(unit)
        order, gather = UNITS[unit][1:]
        made = []
        for k in NEAR_FIRST:
            if stage < 3:
                axis = order[stage]
                src = (P, Q1, Q2)[stage].at[cut(unit, stage, (me[axis] + k) % 4)]
                dst = (R1.at[k - 1], R2.at[k - 1], RA.at[0, k - 1])[stage]
            else:
                axis = gather[stage - 3]
                if stage == 3:
                    src = RA.at[1 + me["y"], me["z"]]
                elif axis == "y":
                    src = RA.at[1 + me["y"]]
                else:
                    src = RA.at[pl.ds(1, 4), me["z"]]
                dst = src
            made.append(pltpu.make_async_remote_copy(
                src_ref=src, dst_ref=dst, send_sem=s.at[unit, stage, k - 1], recv_sem=r.at[unit, stage, k - 1],
                device_id=peer(axis, k), device_id_type=MESH))
        return made

    def start(unit, stage):
        for copy in copies(unit, stage):
            copy.start()

    def wait(unit, stage):
        for copy in copies(unit, stage):
            copy.wait_recv()

    def out_copies(unit):
        RA = buffers(unit)[7]
        made = []
        if unit < 2:
            base, rows = 256 * unit, UNITS[unit][0][0]
            for y in range(4):
                for z in range(4 if unit == 0 else 3):
                    made.append((RA.at[1 + y, z], d_out.at[pl.ds(base + z * rows, rows), pl.ds(y * 256, 256)]))
        else:
            columns = pl.ds(*CHUNKS[unit - 2])
            for y in range(4):
                out = (g_out, u_out)[y // 2]
                made += [(RA.at[1 + y, z], out.at[pl.ds((y % 2) * 64 + z * 16, 16), columns]) for z in range(4)]
        return [pltpu.make_async_copy(src, dst, out_sem.at[unit, n]) for n, (src, dst) in enumerate(made)]

    def advance(unit, stage):
        P, R1, Q1, F1, R2, Q2, F2, RA = buffers(unit)
        wait(unit, stage)
        if stage < 3:
            axis = UNITS[unit][1][stage]
            mine = (P, F1, F2)[stage][cut(unit, stage, me[axis])].astype(F32)
            for k in range(3):
                mine += (R1[k] if stage == 0 else R2[k] if stage == 1 else RA[0, k]).astype(F32)
            if stage == 0:
                F1[...], Q1[...] = mine, mine.astype(BF)
            elif stage == 1:
                F2[...], Q2[...] = mine, mine.astype(BF)
            else:
                RA[1 + me["y"], me["z"]] = mine.astype(BF)
        if stage < 4:
            start(unit, stage + 1)
        else:
            for copy in out_copies(unit):
                copy.start()

    B, C, E, G1, G2 = range(5)
    after = {
        0: [("go", 2)],
        1: [("go", 3)],
        2: [("go", 4), (1, B)],
        3: [("go", 5), (2, B), (0, B), (1, C)],
        4: [("go", 6), (3, B), (2, C), (0, C), (1, E)],
        5: [("go", 7), (4, B), (5, B), (3, C), (2, E), (0, E), (1, G1)],
        6: [("go", 8), (4, C), (5, C), (3, E), (2, G1), (0, G1), (1, G2),
            (4, E), (5, E), (3, G1), (2, G2), (0, G2),
            (6, B), (7, B), (8, B), (4, G1), (5, G1), (3, G2),
            (6, C), (7, C), (8, C), (4, G2), (5, G2),
            (6, E), (7, E), (8, E), (6, G1), (7, G1), (8, G1), (6, G2), (7, G2), (8, G2)],
    }

    def run(tick):
        for what in after[tick]:
            if what[0] == "go":
                start(what[1], 0)
            else:
                advance(*what)

    def parity(half):
        return core if half else 1 - core

    def hid_copy(j):
        block = 2 * (j % 4) + jnp.where(j < 4, 1 - core, core)
        rows = pl.ds(pl.multiple_of(block * 400, 16), 400)
        return pltpu.make_async_copy(hidT.at[rows], hid.at[j % 2], hid_sem.at[j % 2])

    def y_copy(half):
        return pltpu.make_async_copy(by_y.at[:, pl.ds(half * 512, 512)], rhs.at[1, half], y_sem.at[half])

    def rhs_copy(n, mat):
        columns = pl.ds(pl.multiple_of(n * 512, 512), 512)
        return pltpu.make_async_copy((dg, du)[mat].at[:, columns], rhs.at[n % 2, mat], rhs_sem.at[n % 2, mat])

    def tail_copy(mat):
        return pltpu.make_async_copy((dg, du)[mat].at[:, pl.ds(3072, 128)], rhs_tail.at[mat], tail_sem.at[mat])

    PA, PB = buffers(0)[0], buffers(1)[0]

    def pair_d(k, which):
        src, dst = ((send_d, PA), (send_e, PB))[which]
        return pltpu.make_async_remote_copy(
            src_ref=src.at[k], dst_ref=dst.at[k], send_sem=pair_s.at[k, which], recv_sem=pair_r.at[k, which],
            device_id=partner, device_id_type=MESH)

    hid_copy(0).start()
    for half in range(2):
        y_copy(half).start()

    def a_copy(half, x):
        rows = pl.ds(pl.multiple_of((2 * x + parity(half)) * 128, 128), 128)
        return pltpu.make_async_copy(aT.at[rows], a.at[half, pl.ds(x * 128, 128)], a_sem.at[half, x])

    for half in range(2):
        for x in range(4):
            a_copy(half, x).start()
    for mat in range(2):
        rhs_copy(0, mat).start()
        tail_copy(mat).start()
    send_e[:, :, pl.ds(3, 1)] = jnp.zeros((4, 4, 1, 48, 256), BF)
    for half in range(2):
        y_copy(half).wait()

    def down_step(j, carry):
        hid_copy(j).wait()

        @pl.when(j < 7)
        def _():
            hid_copy(j + 1).start()

        k = j % 4
        for half in range(2):
            out = dot(hid[j % 2], rhs[1, half])
            upper = [out[:256, 256 * n : 256 * n + 256].reshape(4, 64, 256) for n in range(2)]
            lower = [out[256:, 256 * n : 256 * n + 256].reshape(3, 48, 256) for n in range(2)]
            if half == 0:

                @pl.when(j >= 4)
                def _():
                    pair_d(k, 0).wait_recv()
                    pair_d(k, 1).wait_recv()

            for n in range(2):
                y = 2 * half + n

                @pl.when(j < 4)
                def _():
                    send_d[k, y] = upper[n].astype(BF)
                    send_e[k, y, pl.ds(0, 3)] = lower[n].astype(BF)

                @pl.when(j >= 4)
                def _():
                    PA[k, y] = (PA[k, y].astype(F32) + upper[n]).astype(BF)
                    PB[k, y, pl.ds(0, 3)] = (PB[k, y, pl.ds(0, 3)].astype(F32) + lower[n]).astype(BF)

        @pl.when(j < 4)
        def _():
            pair_d(k, 0).start()
            pair_d(k, 1).start()

        return carry

    lax.fori_loop(0, 8, down_step, 0)
    for unit in range(2):
        start(unit, 0)
    for mat in range(2):
        rhs_copy(1, mat).start()
    for half in range(2):
        for x in range(4):
            a_copy(half, x).wait()

    def gate_up(P, send, rights, pair, columns):
        for mat in range(2):
            send[:, pl.ds(2 * mat, 2)] = dot(a[0], rights(mat)).astype(BF).reshape(4, 2, 4, 16, columns)
        pair.start()
        own = [dot(a[1], rights(mat)).reshape(4, 2, 4, 16, columns) for mat in range(2)]
        pair.wait_recv()
        for mat in range(2):
            part = pl.ds(2 * mat, 2)
            P[:, part] = (P[:, part].astype(F32) + own[mat]).astype(BF)

    def pair_u(n):
        return pltpu.make_async_remote_copy(
            src_ref=send_u.at[n % 2], dst_ref=bufs[16].at[n], send_sem=pair_s.at[4 + n, 0], recv_sem=pair_r.at[4 + n, 0],
            device_id=partner, device_id_type=MESH)

    pair_t = pltpu.make_async_remote_copy(
        src_ref=send_t, dst_ref=buffers(8)[0], send_sem=pair_s.at[10, 0], recv_sem=pair_r.at[10, 0],
        device_id=partner, device_id_type=MESH)

    def chunk_step(n, carry):
        for mat in range(2):
            rhs_copy(n, mat).wait()

        @pl.when(n >= 2)
        def _():
            pair_u(n - 2).wait_send()

        gate_up(bufs[16].at[n], send_u.at[n % 2], lambda mat: rhs[n % 2, mat], pair_u(n), 512)

        @pl.when(n < 4)
        def _():
            for mat in range(2):
                rhs_copy(n + 2, mat).start()

        for tick in range(6):

            @pl.when(n == tick)
            def _():
                run(tick)

        return carry

    lax.fori_loop(0, 6, chunk_step, 0)
    for mat in range(2):
        tail_copy(mat).wait()
    gate_up(buffers(8)[0], send_t, lambda mat: rhs_tail[mat], pair_t, 128)
    run(6)

    for k in range(4):
        for which in range(2):
            pair_d(k, which).wait_send()
    for n in (4, 5):
        pair_u(n).wait_send()
    pair_t.wait_send()
    for unit in range(len(UNITS)):
        for stage in range(5):
            for copy in copies(unit, stage):
                copy.wait_send()
        for copy in out_copies(unit):
            copy.wait()


def gradients(number, aT, hidT, dg, du, by_y):
    dma = pltpu.SemaphoreType.DMA
    bufs = []
    for first, count in KINDS:
        tile = UNITS[first][0]
        bufs += [
            pltpu.VMEM((count, 4, 4, 4) + tile, BF),
            pltpu.VMEM((count, 3, 4, 4) + tile, BF),
            pltpu.VMEM((count, 4, 4) + tile, BF),
            pltpu.VMEM((count, 4, 4) + tile, F32),
            pltpu.VMEM((count, 3, 4) + tile, BF),
            pltpu.VMEM((count, 4) + tile, BF),
            pltpu.VMEM((count, 4) + tile, F32),
            pltpu.VMEM((count, 5, 4) + tile, BF),
        ]
    return pl.pallas_call(
        gradients_kernel,
        out_shape=(
            jax.ShapeDtypeStruct((128, FF), BF),
            jax.ShapeDtypeStruct((128, FF), BF),
            jax.ShapeDtypeStruct((400, D), BF),
        ),
        in_specs=[ANY] * 5,
        out_specs=(ANY,) * 3,
        scratch_shapes=[
            pltpu.VMEM((2, 512, T), BF),
            pltpu.VMEM((2, 2, T, 512), BF),
            pltpu.VMEM((2, T, 128), BF),
            pltpu.VMEM((2, 400, T), BF),
            pltpu.VMEM((4, 4, 4, 64, 256), BF),
            pltpu.VMEM((4, 4, 4, 48, 256), BF),
            pltpu.VMEM((2, 4, 4, 4, 16, 512), BF),
            pltpu.VMEM((4, 4, 4, 16, 128), BF),
            *bufs,
            dma((11, 2)), dma((11, 2)), dma((9, 5, 3)), dma((9, 5, 3)), dma((2, 4)), dma((2, 2)), dma((2,)), dma((2,)), dma((2,)), dma((9, 16)),
        ],
        compiler_params=pltpu.CompilerParams(collective_id=1 + number, has_side_effects=True, vmem_limit_bytes=VMEM_LIMIT),
        cost_estimate=cost(3, 60_000_000),
        name=f"gradients_{number}",
    )(aT, hidT, dg, du, by_y)


def adamw(w, m, v, g):
    m = 0.9 * m + 0.1 * g
    v = 0.95 * v + 0.05 * g * g
    step = m * lax.rsqrt(v + 1e-8) + 0.1 * w
    return (w - 0.02 * step).astype(BF), m, v


def solution(mesh):
    def step(x, dy, *arrays):
        weights, m, v = (arrays[i : i + 3] for i in (0, 3, 6))
        x, dy = x[0], dy[0]
        G, U, Dn, hid0, a0, h1 = forward(x, *weights)
        hid1, a1, dg1, du1 = hidden(1, True, h1, dy, G, U, Dn)
        one = gradients(1, a1, hid1, dg1, du1, dy)
        by_h1 = input_gradient(1, h1, dy, dg1, du1, G, U)
        dg0, du0 = hidden(0, False, x, by_h1, G, U, Dn)
        zero = gradients(0, a0, hid0, dg0, du0, by_h1)
        summed = [jnp.stack(pair).astype(F32) for pair in zip(zero, one, strict=True)]
        new = [adamw(w.astype(F32), m, v, g) for w, m, v, g in zip(weights, m, v, summed, strict=True)]
        return tuple(one[which] for which in range(3) for one in new)

    states, cut = P(("rep", "r", "s"), None, None), P(None, "s", None)
    return jax.shard_map(
        step,
        mesh=mesh,
        in_specs=(states, states) + (cut,) * 9,
        out_specs=(P("rep", "s", None),) * 9,
        check_vma=False,
    )
```

time: 807 us -> 572 us (0.71)
  Pallas kernels: 0 us -> 544 us
  matrix products: 373 us -> 0 us
  waiting for transfers between devices: 360 us -> 0 us
  local copies, waits for them, and re-layouts: 26.5 us -> 1.15 us
  between operations: 14.3 us -> 0.95 us
    pallas_call x0 -> x6, Pallas kernels: none -> 544 us  [the longest x2 269 us: gradients(): pl.pallas_call(gradients_kernel, out_shape=(jax.ShapeDtypeStruct((128, FF...]
    dot_general x15 -> x0, matrix products: 373 us -> none  [the longest x5 137 us: layer(): gate = jnp.dot(a, w['w_gate'], preferred_element_type=jnp.float32)]
    all_gather x6 -> x0, waiting for transfers between devices: 123 us -> none  [fetched(): lax.all_gather(w[number], 's', axis=0, tiled=True)]
    reduce_scatter x6 -> x0, waiting for transfers between devices: 121 us -> none  [summed(): lax.psum_scatter(term, 's', scatter_dimension=0, tiled=True)]
    psum x1 -> x0, waiting for transfers between devices: 114 us -> none  [summed(): lax.psum(lax.psum_scatter(term, 's', scatter_dimension=0, tiled=True), 'r')]
    unnamed x42 -> x12, local copies, waits for them, and re-layouts: 19.8 us -> 1.15 us
  transfers between devices with their start and end apart: 13 -> 0, of which waited for: 10 -> 0; matrix products, arithmetic and copies ran while one was open for 36% -> 0% of each run, Pallas kernels for 0% -> 0%
where the time goes in v1:
time: 572 us; the launch traced here: 564 us
  Pallas kernels  544 us (95%)
  other arithmetic  17.8 us (3%)
    pallas_call x2, Pallas kernels, gradients(): pl.pallas_call(gradients_kernel, out_shape=(jax.ShapeDtypeStruct((128, FF...  269 us
    pallas_call x2, Pallas kernels, hidden(): pl.pallas_call(functools.partial(hidden_kernel, number, want_hid), grid=(...  120 us
    pallas_call x1, Pallas kernels, forward(): pl.pallas_call(forward_kernel, out_shape=(jax.ShapeDtypeStruct((2, 8, 128...  113 us
    pallas_call x1, Pallas kernels, input_gradient(): pl.pallas_call(functools.partial(input_kernel, number), grid=(T // TM,),...  42.2 us
    convert_element_type x2, other arithmetic, adamw(): return ((w - 0.02 * step).astype(BF), m, v)  17.8 us

profile of v1, /device:TPU:0, one launch (start us, length us, event | category | flops | bytes accessed | tf_op | source)
XLA Modules:
  0.0 563.6 jit_solution(4455666114394912860)
XLA Ops:
  0.6 113.1 %forward.1 = (bf16[2,8,128,3200]{3,2,1,0:T(8,128)(2,1)}, bf16[2,8,128,3200]{3,2,1,0:T(8,128)(2,1)}, bf16[2,8,400,1024]{3,2,1,0:T(8,128)(2,1)}, bf16[3200,2048]{1...) custom-call(bf16[2048,1024]{1,0:T(8,128)(2,1)} %bitcast.20, bf16[2,128,3200]{2,1,0:T(8,128)(2,1)} %g_hbm.1, ...), custom_call_target="tpu_custom_call" | custom-call | flops 40265318400 | bytes 60000000 | tf_op jit(solution)/shard_map/forward/pallas_call | solution.py:257
  113.7 62.0 %hidden_1.1 = (bf16[3200,2048]{1,0:T(8,128)(2,1)}, bf16[1024,2048]{1,0:T(8,128)(2,1)}, bf16[2048,3200]{1,0:T(8,128)(2,1)}, bf16[2048,3200]{1,0:T(8,128)(2,1)}) custom-call(bf16[2048,1024]{1,0:T(8,128)(2,1)} %get-tuple-element.29.h, bf16[2048,1024]{1,0:T(8,128)(2,1)} %bitcast.17, bf16[2,1024,3200]{2,1,0:T(8,128)(2,1)} %bitcast.22, ...), custom_call_target="tpu_custom_call" | custom-call | flops 40265318400 | bytes 70000000 | tf_op jit(solution)/shard_map/hidden_1/pallas_call | solution.py:341
  175.7 134.6 %gradients_1.1 = (bf16[128,3200]{1,0:T(8,128)(2,1)}, bf16[128,3200]{1,0:T(8,128)(2,1)}, bf16[400,1024]{1,0:T(8,128)(2,1)}) custom-call(bf16[1024,2048]{1,0:T(8,128)(2,1)} %get-tuple-element.38.aT, bf16[3200,2048]{1,0:T(8,128)(2,1)} %get-tuple-element.39.hidT, bf16[2048,3200]{1,0:T(8,128)(2,1)} %get-tuple-element.33.dg, ...), custom_call_target="tpu_custom_call" | custom-call | flops 40265318400 | bytes 60000000 | tf_op jit(solution)/shard_map/gradients_1/pallas_call | solution.py:707
  310.3 42.2 %input_1.1.by_y = bf16[2048,1024]{1,0:T(8,128)(2,1)} custom-call(bf16[2048,1024]{1,0:T(8,128)(2,1)} %get-tuple-element.29.h, bf16[2048,1024]{1,0:T(8,128)(2,1)} %bitcast.19, bf16[2048,3200]{1,0:T(8,128)(2,1)} %get-tuple-element.33.dg, bf16[2048,3200]{1,0:T(8,128)(2,1)} %get-tuple-element.34.du, bf16[2,1024,3200]{2,1,0:T(8,128)(2,1)} %bitcast.23, ...), custom_call_target="tpu_custom_call" | custom-call | flops 26843545600 | bytes 50000000 | tf_op jit(solution)/shard_map/input_1/pallas_call | solution.py:387
  352.6 57.6 %hidden_0.1 = (bf16[2048,3200]{1,0:T(8,128)(2,1)}, bf16[2048,3200]{1,0:T(8,128)(2,1)}) custom-call(bf16[2048,1024]{1,0:T(8,128)(2,1)} %bitcast.21, bf16[2048,1024]{1,0:T(8,128)(2,1)} %input_1.1.by_y, bf16[2,1024,3200]{2,1,0:T(8,128)(2,1)} %bitcast.24, bf16[2,1024,3200]{2,1,0:T(8,128)(2,1)} %bitcast.27, bf16[2,3200,1024]{2,1,0:T(8,128)(2,1)} %bitcast.29), custom_call_target="tpu_custom_call" | custom-call | flops 40265318400 | bytes 70000000 | tf_op jit(solution)/shard_map/hidden_0/pallas_call | solution.py:341
  410.2 0.0 copy-start.4
  410.2 134.1 %gradients_0.1 = (bf16[128,3200]{1,0:T(8,128)(2,1)}, bf16[128,3200]{1,0:T(8,128)(2,1)}, bf16[400,1024]{1,0:T(8,128)(2,1)}) custom-call(bf16[1024,2048]{1,0:T(8,128)(2,1)} %get-tuple-element.27.aT, bf16[3200,2048]{1,0:T(8,128)(2,1)} %get-tuple-element.28.hidT, bf16[2048,3200]{1,0:T(8,128)(2,1)} %get-tuple-element.35.dg, ...), custom_call_target="tpu_custom_call" | custom-call | flops 40265318400 | bytes 60000000 | tf_op jit(solution)/shard_map/gradients_0/pallas_call | solution.py:707
  544.4 0.0 copy-done.4
  544.4 0.0 copy-start
  544.4 0.0 copy-start.1
  544.4 0.0 copy-start.2
  544.4 0.0 copy-start.3
  544.4 0.0 copy-start.5
  544.4 13.6 %fusion.2 = (bf16[2,128,3200]{2,1,0:T(8,128)(2,1)}, f32[2,128,3200]{2,1,0:T(8,128)}, f32[2,128,3200]{2,1,0:T(8,128)}, bf16[2,128,3200]{2,1,0:T(8,128)(2,1)}, f32...) fusion(bf16[2,128,3200]{2,1,0:T(8,128)(2,1)} %g_hbm.1, bf16[1,128,3200]{2,1,0:T(8,128)(2,1)S(1)} %bitcast.12, ...), kind=kLoop, calls=%fused_computation.14 | loop fusion | flops 31129600 | bytes 36044800 | tf_op jit(solution)/shard_map/convert_element_type | solution.py:738
  558.1 0.0 copy-done
  558.1 0.0 copy-done.1
  558.1 0.2 copy-done.2
  558.3 0.7 copy-done.3
  559.0 0.2 copy-done.5
  559.2 4.2 fusion.10
Async XLA Ops:
  410.2 134.1 %copy-start.4 = (bf16[128,3200]{1,0:T(8,128)(2,1)S(1)}, bf16[128,3200]{1,0:T(8,128)(2,1)}, u32[]{:S(2)}) copy-start(bf16[128,3200]{1,0:T(8,128)(2,1)} %get-tuple-element.40) | copy-start | bytes 2457604
  544.4 13.7 %copy-start = (f32[2,400,1024]{2,1,0:T(8,128)S(1)}, f32[2,400,1024]{2,1,0:T(8,128)}, u32[]{:S(2)}) copy-start(f32[2,400,1024]{2,1,0:T(8,128)} %param.21) | copy-start | bytes 9830404
  544.4 13.7 %copy-start.1 = (f32[2,400,1024]{2,1,0:T(8,128)S(1)}, f32[2,400,1024]{2,1,0:T(8,128)}, u32[]{:S(2)}) copy-start(f32[2,400,1024]{2,1,0:T(8,128)} %param.18) | copy-start | bytes 9830404
  544.4 13.9 %copy-start.2 = (bf16[2,400,1024]{2,1,0:T(8,128)(2,1)S(1)}, bf16[2,400,1024]{2,1,0:T(8,128)(2,1)}, u32[]{:S(2)}) copy-start(bf16[2,400,1024]{2,1,0:T(8,128)(2,1)} %d_hbm.1) | copy-start | bytes 4915204
  544.4 14.6 %copy-start.3 = (bf16[400,1024]{1,0:T(8,128)(2,1)S(1)}, bf16[400,1024]{1,0:T(8,128)(2,1)}, u32[]{:S(2)}) copy-start(bf16[400,1024]{1,0:T(8,128)(2,1)} %get-tuple-element.44) | copy-start | bytes 2457604
  544.4 14.8 %copy-start.5 = (bf16[400,1024]{1,0:T(8,128)(2,1)S(1)}, bf16[400,1024]{1,0:T(8,128)(2,1)}, u32[]{:S(2)}) copy-start(bf16[400,1024]{1,0:T(8,128)(2,1)} %get-tuple-element.43) | copy-start | bytes 2457604

commit v2 on v1

--- a/solution.py
+++ b/solution.py
@@ -11,8 +11,11 @@
 MESH = pl.DeviceIdType.MESH
 VMEM_LIMIT = 66_000_000
 T, D, FF = 2048, 1024, 3200
-TM = 512
-CHUNKS = tuple((512 * j, 512) for j in range(6)) + ((3072, 128),)
+WAY = 4
+OWN = 400
+TILE, LANES, SIDE, WIDE = 16, 128, 256, 512
+TM = WIDE
+CHUNKS = tuple((WIDE * j, WIDE) for j in range(6)) + ((3072, LANES),)
 GROUPS = ((0, 1024), (1024, 2176))
 ANY = pl.BlockSpec(memory_space=pl.ANY)
 
@@ -46,17 +49,17 @@
     s1, r1, s2, r2, s3, r3, stage_sem, own_sem, x_sem, w_sem, hid_sem, a_sem, h_sem,
 ):
     r, s = lax.axis_index("r"), lax.axis_index("s")
-    y, z = r // 4, r % 4
+    y, z = r // WAY, r % WAY
     cx, core = s // 2, s % 2
 
     def at_x(k):
-        return {"r": r, "s": 2 * ((cx + k) % 4) + core}
+        return {"r": r, "s": 2 * ((cx + k) % WAY) + core}
 
     def at_y(k):
-        return {"r": ((y + k) % 4) * 4 + z, "s": s}
+        return {"r": ((y + k) % WAY) * WAY + z, "s": s}
 
     def at_z(k):
-        return {"r": y * 4 + (z + k) % 4, "s": s}
+        return {"r": y * WAY + (z + k) % WAY, "s": s}
 
     partner = {"r": r, "s": s + 1 - 2 * core}
 
@@ -65,18 +68,26 @@
         pl.semaphore_signal(barrier, inc=1, device_id=to, device_id_type=MESH)
     pl.semaphore_wait(barrier, 10)
 
-    mats = [m for l in range(2) for m in ((g_hbm, l, G, stage_g, 128), (u_hbm, l, U, stage_u, 128), (d_hbm, l, Dn, stage_d, 400))]
+    mats = [m for l in range(2) for m in ((g_hbm, l, G, stage_g, LANES), (u_hbm, l, U, stage_u, LANES), (d_hbm, l, Dn, stage_d, OWN))]
 
     def piece(rows, half, j):
-        if rows == 128:
-            return pl.ds(pl.multiple_of(half * 64 + j * 16, 16), 16), slice(None)
-        return slice(None), pl.ds(pl.multiple_of(half * 512 + j * 128, 128), 128)
+        if rows == LANES:
+            return pl.ds(pl.multiple_of(half * 64 + j * TILE, TILE), TILE), slice(None)
+        return slice(None), pl.ds(pl.multiple_of(half * WIDE + j * LANES, LANES), LANES)
 
     def block(whole, l, b, rows, half=None, j=None):
         if half is None:
             return whole.at[l, b]
         p = piece(rows, half, j)
         return whole.at[l, b, p[0], p[1]]
+
+    def halved(ref, rows, back):
+        if rows == LANES:
+            return ref.at[:, pl.ds(1664 * back, 1664 - LANES * back)]
+        return ref.at[pl.ds(208 * back, 208 - TILE * back), :]
+
+    def source(k):
+        return 2 * ((cx + WAY - k) % WAY) + core
 
     def c1(i, half, k):
         shard, l, whole, _, rows = mats[i]
@@ -84,19 +95,32 @@
         p = piece(rows, half, j)
         return pltpu.make_async_remote_copy(
             src_ref=shard.at[l, p[0], p[1]], dst_ref=block(whole, l, s, rows, half, j),
-            send_sem=s1.at[i, half, k - 1], recv_sem=r1.at[i, half, k - 1], device_id=at_x(k), device_id_type=MESH)
+            send_sem=s1.at[i, half, k // 2], recv_sem=r1.at[i, half, k // 2], device_id=at_x(k), device_id_type=MESH)
+
+    def f1(i, half, k):
+        _, l, whole, _, rows = mats[i]
+        ref = halved(block(whole, l, source(k), rows, half, (y, z)[half]), rows, k // 2)
+        return pltpu.make_async_remote_copy(
+            src_ref=ref, dst_ref=ref, send_sem=s1.at[i, half, 2 + k // 2], recv_sem=r1.at[i, half, 2 + k // 2],
+            device_id=at_x(k), device_id_type=MESH)
 
     def c2(i, half, k, q):
         _, l, whole, _, rows = mats[i]
-        b = 2 * ((cx + 4 - k) % 4) + core
-        ref = block(whole, l, b, rows, half, (y, z)[half])
+        ref = block(whole, l, source(k), rows, half, (y, z)[half])
         return pltpu.make_async_remote_copy(
-            src_ref=ref, dst_ref=ref, send_sem=s2.at[i, half, k - 1, q - 1], recv_sem=r2.at[i, half, k - 1, q - 1],
+            src_ref=ref, dst_ref=ref, send_sem=s2.at[i, half, k - 1, q // 2], recv_sem=r2.at[i, half, k - 1, q // 2],
+            device_id=(at_y, at_z)[half](q), device_id_type=MESH)
+
+    def f2(i, half, k, q):
+        _, l, whole, _, rows = mats[i]
+        ref = halved(block(whole, l, source(k), rows, half, ((y, z)[half] + WAY - q) % WAY), rows, q // 2)
+        return pltpu.make_async_remote_copy(
+            src_ref=ref, dst_ref=ref, send_sem=s2.at[i, half, k - 1, 2 + q // 2], recv_sem=r2.at[i, half, k - 1, 2 + q // 2],
             device_id=(at_y, at_z)[half](q), device_id_type=MESH)
 
     def c3(i, k):
         shard, l, whole, _, rows = mats[i]
-        b = 2 * ((cx + 4 - k) % 4) + core
+        b = source(k)
         src = shard.at[l] if k == 0 else whole.at[l, b]
         return pltpu.make_async_remote_copy(
             src_ref=src, dst_ref=whole.at[l, b], send_sem=s3.at[i, k], recv_sem=r3.at[i, k], device_id=partner, device_id_type=MESH)
@@ -109,30 +133,49 @@
         _, l, whole, stage, _ = mats[i]
         return pltpu.make_async_copy(stage.at[l], whole.at[l, s], own_sem.at[i])
 
-    near_first = (1, 3, 2)
+    sides, halves = (1, 3), range(2)
 
     def p1(i):
-        for k in near_first:
-            for half in range(2):
+        for k in sides:
+            for half in halves:
                 c1(i, half, k).start()
         c3(i, 0).start()
 
     def p2(i):
-        for k in near_first:
-            for half in range(2):
+        for k in sides:
+            for half in halves:
                 c1(i, half, k).wait_recv()
-                for q in near_first:
+                f1(i, half, k).start()
+                for q in sides:
                     c2(i, half, k, q).start()
 
+    def p2b(i):
+        for half in halves:
+            for k in sides:
+                f1(i, half, k).wait_recv()
+            for q in sides:
+                c2(i, half, 2, q).start()
+        for k in sides:
+            for half in halves:
+                for q in sides:
+                    c2(i, half, k, q).wait_recv()
+                    f2(i, half, k, q).start()
+
+    def p2c(i):
+        for half in halves:
+            for q in sides:
+                c2(i, half, 2, q).wait_recv()
+                f2(i, half, 2, q).start()
+
     def p3(i):
-        for k in near_first:
-            for half in range(2):
-                for q in near_first:
-                    c2(i, half, k, q).wait_recv()
+        for k in (1, 3, 2):
+            for half in halves:
+                for q in sides:
+                    f2(i, half, k, q).wait_recv()
             c3(i, k).start()
 
     def arrived(i):
-        for k in range(4):
+        for k in range(WAY):
             c3(i, k).wait_recv()
 
     loads = {0: wg, 1: wu, 2: wd}
@@ -162,12 +205,18 @@
         stage_out(i).start()
     p2(0)
     p2(1)
+    p2b(0)
+    p2c(0)
+    p2(2)
+    p2b(1)
     p3(0)
-    p2(2)
+    p2c(1)
     p2(3)
     load_start(0)
+    p2b(2)
     p3(1)
-    p2(4)
+    p2c(2)
+    p2(WAY)
     load_start(1)
     x_copy.wait()
     load_wait(0)
@@ -207,16 +256,26 @@
         @pl.when(m == 0)
         def _():
             p2(5)
+            p2b(3)
             p3(2)
+            p2c(3)
+            p2b(WAY)
 
         @pl.when(m == 1)
         def _():
             p3(3)
             load_start(2)
+            p2c(WAY)
+            p2b(5)
 
         @pl.when(m == 2)
         def _():
-            p3(4)
+            p3(WAY)
+            p2c(5)
+
+        @pl.when(m == 3)
+        def _():
+            p3(5)
 
         return carry
 
@@ -224,31 +283,29 @@
         out = dot(hid[rows_of(m), :], wd[...]).astype(BF)
         x[rows_of(m), :] = (x[rows_of(m), :].astype(F32) + out.astype(F32)).astype(BF)
         h_copy(m).start()
-
-        @pl.when(m == 1)
-        def _():
-            p3(5)
-
         return carry
 
-    lax.fori_loop(0, 4, up_step, 0)
+    lax.fori_loop(0, WAY, up_step, 0)
     load_wait(2)
-    lax.fori_loop(0, 4, down_step, 0)
+    lax.fori_loop(0, WAY, down_step, 0)
 
     for i in range(6):
         if i > 2:
             arrived(i)
             stage_out(i).wait()
-        for k in (1, 2, 3):
-            for half in range(2):
+        for half in halves:
+            for k in sides:
                 c1(i, half, k).wait_send()
-                for q in (1, 2, 3):
+                f1(i, half, k).wait_send()
+            for k in (1, 2, 3):
+                for q in sides:
                     c2(i, half, k, q).wait_send()
-        for k in range(4):
+                    f2(i, half, k, q).wait_send()
+        for k in range(WAY):
             c3(i, k).wait_send()
     hid_copy(3).wait()
     a_copy(3).wait()
-    for m in range(4):
+    for m in range(WAY):
         h_copy(m).wait()
 
 
@@ -257,20 +314,20 @@
     return pl.pallas_call(
         forward_kernel,
         out_shape=(
-            jax.ShapeDtypeStruct((2, 8, 128, FF), BF),
-            jax.ShapeDtypeStruct((2, 8, 128, FF), BF),
-            jax.ShapeDtypeStruct((2, 8, 400, D), BF),
+            jax.ShapeDtypeStruct((2, 8, LANES, FF), BF),
+            jax.ShapeDtypeStruct((2, 8, LANES, FF), BF),
+            jax.ShapeDtypeStruct((2, 8, OWN, D), BF),
             jax.ShapeDtypeStruct((FF, T), BF),
             jax.ShapeDtypeStruct((D, T), BF),
             jax.ShapeDtypeStruct((T, D), BF),
         ),
-        in_specs=[ANY] * 4,
+        in_specs=[ANY] * WAY,
         out_specs=(ANY,) * 6,
         scratch_shapes=[
             pltpu.VMEM((T, D), BF),
-            pltpu.VMEM((2, 128, FF), BF),
-            pltpu.VMEM((2, 128, FF), BF),
-            pltpu.VMEM((2, 400, D), BF),
+            pltpu.VMEM((2, LANES, FF), BF),
+            pltpu.VMEM((2, LANES, FF), BF),
+            pltpu.VMEM((2, OWN, D), BF),
             pltpu.VMEM((D, FF), BF),
             pltpu.VMEM((D, FF), BF),
             pltpu.VMEM((FF, D), BF),
@@ -278,8 +335,8 @@
             pltpu.VMEM((TM, D), BF),
             pltpu.VMEM((D, TM), BF),
             pltpu.VMEM((FF, TM), BF),
-            dma((6, 2, 3)), dma((6, 2, 3)), dma((6, 2, 3, 3)), dma((6, 2, 3, 3)), dma((6, 4)), dma((6, 4)),
-            dma((6,)), dma((6,)), dma, dma((3, 8)), dma((4,)), dma((4,)), dma((4,)),
+            dma((6, 2, WAY)), dma((6, 2, WAY)), dma((6, 2, 3, WAY)), dma((6, 2, 3, WAY)), dma((6, WAY)), dma((6, WAY)),
+            dma((6,)), dma((6,)), dma, dma((3, 8)), dma((WAY,)), dma((WAY,)), dma((WAY,)),
         ],
         compiler_params=pltpu.CompilerParams(collective_id=0, has_side_effects=True, vmem_limit_bytes=VMEM_LIMIT),
         cost_estimate=cost(3, 60_000_000),
@@ -398,17 +455,17 @@
 
 
 UNITS = (
-    ((64, 256), "yxz", "zy"),
-    ((48, 256), "zxy", "yz"),
-    ((16, 512), "xyz", "zy"),
-    ((16, 512), "xzy", "yz"),
-    ((16, 512), "yxz", "zy"),
-    ((16, 512), "xzy", "yz"),
-    ((16, 512), "xyz", "zy"),
-    ((16, 512), "zxy", "yz"),
-    ((16, 128), "xyz", "yz"),
+    ((64, SIDE), "yxz", "zy"),
+    ((48, SIDE), "zxy", "yz"),
+    ((TILE, WIDE), "xyz", "zy"),
+    ((TILE, WIDE), "xzy", "yz"),
+    ((TILE, WIDE), "yxz", "zy"),
+    ((TILE, WIDE), "xzy", "yz"),
+    ((TILE, WIDE), "xyz", "zy"),
+    ((TILE, WIDE), "zxy", "yz"),
+    ((TILE, LANES), "xyz", "yz"),
 )
-NEAR_FIRST = (1, 3, 2)
+SIDES, NEAR_FIRST = (1, 3), (1, 3, 2)
 KINDS = ((0, 1), (1, 1), (2, 6), (8, 1))
 
 
@@ -420,14 +477,14 @@
     bufs, (pair_s, pair_r, s, r, a_sem, rhs_sem, tail_sem, hid_sem, y_sem, out_sem) = rest[:32], rest[32:]
     ri, si = lax.axis_index("r"), lax.axis_index("s")
     core = si % 2
-    me = {"x": si // 2, "y": ri // 4, "z": ri % 4}
+    me = {"x": si // 2, "y": ri // WAY, "z": ri % WAY}
 
     def peer(axis, k):
         if axis == "x":
-            return {"r": ri, "s": 2 * ((me["x"] + k) % 4) + core}
+            return {"r": ri, "s": 2 * ((me["x"] + k) % WAY) + core}
         if axis == "y":
-            return {"r": ((me["y"] + k) % 4) * 4 + me["z"], "s": si}
-        return {"r": me["y"] * 4 + (me["z"] + k) % 4, "s": si}
+            return {"r": ((me["y"] + k) % WAY) * WAY + me["z"], "s": si}
+        return {"r": me["y"] * WAY + (me["z"] + k) % WAY, "s": si}
 
     partner = {"r": ri, "s": si + 1 - 2 * core}
     barrier = pltpu.get_barrier_semaphore()
@@ -444,114 +501,138 @@
         order = UNITS[unit][1]
         return [axis for axis in "xyz" if axis in order[stage:]]
 
-    def cut(unit, stage, index):
-        return tuple(index if axis == UNITS[unit][1][stage] else slice(None) for axis in others(unit, stage))
-
-    def copies(unit, stage):
+    def cut(unit, stage, index, half=None):
+        axis, index_of = UNITS[unit][1][stage], []
+        for one in others(unit, stage):
+            if one == axis:
+                index_of.append(index)
+            elif half is None:
+                index_of.append(slice(None))
+            else:
+                index_of.append(pl.ds(2 * half, 2))
+                half = None
+        return tuple(index_of)
+
+    def halves_of(RA, axis, index, half=None):
+        part = slice(None) if half is None else pl.ds(2 * half, 2)
+        if axis == "y":
+            return RA.at[1 + index, part]
+        return RA.at[pl.ds(1, WAY) if half is None else pl.ds(1 + 2 * half, 2), index]
+
+    def copies(unit, step):
         P, R1, Q1, F1, R2, Q2, F2, RA = buffers(unit)
         order, gather = UNITS[unit][1:]
         made = []
-        for k in NEAR_FIRST:
-            if stage < 3:
-                axis = order[stage]
-                src = (P, Q1, Q2)[stage].at[cut(unit, stage, (me[axis] + k) % 4)]
-                dst = (R1.at[k - 1], R2.at[k - 1], RA.at[0, k - 1])[stage]
+        for k in NEAR_FIRST if step in (WAY, 5) else SIDES:
+            back = k // 2
+            if step < WAY:
+                stage = step // 2
+                axis, src, dst = order[stage], (P, Q1)[stage], (R1, R2)[stage]
+                if step % 2:
+                    src, dst = src.at[cut(unit, stage, (me[axis] + k) % WAY)], dst.at[back]
+                else:
+                    src, dst = src.at[cut(unit, stage, (me[axis] + 2) % WAY, back)], dst.at[2, pl.ds(2 * back, 2)]
+            elif step == WAY:
+                axis = order[2]
+                src, dst = Q2.at[(me[axis] + k) % WAY], RA.at[0, k - 1]
+            elif step == 5:
+                axis = gather[0]
+                src = dst = RA.at[1 + me["y"], me["z"]]
+            elif step == 6:
+                axis = gather[1]
+                src = dst = halves_of(RA, axis, me[axis])
             else:
-                axis = gather[stage - 3]
-                if stage == 3:
-                    src = RA.at[1 + me["y"], me["z"]]
-                elif axis == "y":
-                    src = RA.at[1 + me["y"]]
-                else:
-                    src = RA.at[pl.ds(1, 4), me["z"]]
-                dst = src
+                axis = gather[1]
+                src = dst = halves_of(RA, axis, (me[axis] + WAY - k) % WAY, back)
             made.append(pltpu.make_async_remote_copy(
-                src_ref=src, dst_ref=dst, send_sem=s.at[unit, stage, k - 1], recv_sem=r.at[unit, stage, k - 1],
+                src_ref=src, dst_ref=dst, send_sem=s.at[unit, step, k - 1], recv_sem=r.at[unit, step, k - 1],
                 device_id=peer(axis, k), device_id_type=MESH))
         return made
 
-    def start(unit, stage):
-        for copy in copies(unit, stage):
+    def start(unit, step):
+        for copy in copies(unit, step):
             copy.start()
 
-    def wait(unit, stage):
-        for copy in copies(unit, stage):
+    def wait(unit, step):
+        for copy in copies(unit, step):
             copy.wait_recv()
 
     def out_copies(unit):
         RA = buffers(unit)[7]
         made = []
         if unit < 2:
-            base, rows = 256 * unit, UNITS[unit][0][0]
-            for y in range(4):
-                for z in range(4 if unit == 0 else 3):
-                    made.append((RA.at[1 + y, z], d_out.at[pl.ds(base + z * rows, rows), pl.ds(y * 256, 256)]))
+            base, rows = SIDE * unit, UNITS[unit][0][0]
+            for y in range(WAY):
+                for z in range(WAY if unit == 0 else 3):
+                    made.append((RA.at[1 + y, z], d_out.at[pl.ds(base + z * rows, rows), pl.ds(y * SIDE, SIDE)]))
         else:
             columns = pl.ds(*CHUNKS[unit - 2])
-            for y in range(4):
+            for y in range(WAY):
                 out = (g_out, u_out)[y // 2]
-                made += [(RA.at[1 + y, z], out.at[pl.ds((y % 2) * 64 + z * 16, 16), columns]) for z in range(4)]
+                made += [(RA.at[1 + y, z], out.at[pl.ds((y % 2) * 64 + z * TILE, TILE), columns]) for z in range(WAY)]
         return [pltpu.make_async_copy(src, dst, out_sem.at[unit, n]) for n, (src, dst) in enumerate(made)]
 
-    def advance(unit, stage):
+    def advance(unit, step):
         P, R1, Q1, F1, R2, Q2, F2, RA = buffers(unit)
-        wait(unit, stage)
-        if stage < 3:
-            axis = UNITS[unit][1][stage]
-            mine = (P, F1, F2)[stage][cut(unit, stage, me[axis])].astype(F32)
+        wait(unit, step)
+        stage = step // 2
+        if step in (0, 2):
+            axis, R, own, to = UNITS[unit][1][stage], (R1, R2)[stage], (P, F1)[stage], (P, Q1)[stage]
+            for k in SIDES:
+                index = cut(unit, stage, (me[axis] + k) % WAY, k // 2)
+                to[index] = (own[index].astype(F32) + R[2, pl.ds(2 * (k // 2), 2)].astype(F32)).astype(BF)
+        elif step in (1, 3):
+            R, own, F, Q = (R1, R2)[stage], (P, F1)[stage], (F1, F2)[stage], (Q1, Q2)[stage]
+            mine = own[cut(unit, stage, me[UNITS[unit][1][stage]])].astype(F32)
+            mine += R[0].astype(F32) + R[1].astype(F32)
+            F[...], Q[...] = mine, mine.astype(BF)
+        elif step == WAY:
+            mine = F2[me[UNITS[unit][1][2]]]
             for k in range(3):
-                mine += (R1[k] if stage == 0 else R2[k] if stage == 1 else RA[0, k]).astype(F32)
-            if stage == 0:
-                F1[...], Q1[...] = mine, mine.astype(BF)
-            elif stage == 1:
-                F2[...], Q2[...] = mine, mine.astype(BF)
-            else:
-                RA[1 + me["y"], me["z"]] = mine.astype(BF)
-        if stage < 4:
-            start(unit, stage + 1)
+                mine += RA[0, k].astype(F32)
+            RA[1 + me["y"], me["z"]] = mine.astype(BF)
+        if step < 7:
+            start(unit, step + 1)
         else:
             for copy in out_copies(unit):
                 copy.start()
 
-    B, C, E, G1, G2 = range(5)
-    after = {
-        0: [("go", 2)],
-        1: [("go", 3)],
-        2: [("go", 4), (1, B)],
-        3: [("go", 5), (2, B), (0, B), (1, C)],
-        4: [("go", 6), (3, B), (2, C), (0, C), (1, E)],
-        5: [("go", 7), (4, B), (5, B), (3, C), (2, E), (0, E), (1, G1)],
-        6: [("go", 8), (4, C), (5, C), (3, E), (2, G1), (0, G1), (1, G2),
-            (4, E), (5, E), (3, G1), (2, G2), (0, G2),
-            (6, B), (7, B), (8, B), (4, G1), (5, G1), (3, G2),
-            (6, C), (7, C), (8, C), (4, G2), (5, G2),
-            (6, E), (7, E), (8, E), (6, G1), (7, G1), (8, G1), (6, G2), (7, G2), (8, G2)],
-    }
+    after = (
+        ("cs",),
+        ("dsb0a0c0",),
+        ("esb1d0",),
+        ("fsa1b2c1e0",),
+        ("gsb3a2c2d1f0",),
+        ("hsb4a3c3d2e1g0h0",),
+        ("isb5a4c4d3e2f1i0", "b6a5c5d4e3f2b7a6c6d5e4f3a7c7", "d6e5f4g1h1i1d7e6f5g2h2i2e7f6", "g3h3i3f7g4h4i4g5h5i5g6h6i6g7h7i7"),
+    )
 
     def run(tick):
         for what in after[tick]:
-            if what[0] == "go":
-                start(what[1], 0)
-            else:
-                advance(*what)
+            for letter, step in zip(what[::2], what[1::2], strict=True):
+                unit = ord(letter) - ord("a")
+                if step == "s":
+                    start(unit, 0)
+                else:
+                    advance(unit, int(step))
 
     def parity(half):
         return core if half else 1 - core
 
     def hid_copy(j):
-        block = 2 * (j % 4) + jnp.where(j < 4, 1 - core, core)
-        rows = pl.ds(pl.multiple_of(block * 400, 16), 400)
+        block = 2 * (j % WAY) + jnp.where(j < WAY, 1 - core, core)
+        rows = pl.ds(pl.multiple_of(block * OWN, TILE), OWN)
         return pltpu.make_async_copy(hidT.at[rows], hid.at[j % 2], hid_sem.at[j % 2])
 
     def y_copy(half):
-        return pltpu.make_async_copy(by_y.at[:, pl.ds(half * 512, 512)], rhs.at[1, half], y_sem.at[half])
+        return pltpu.make_async_copy(by_y.at[:, pl.ds(half * WIDE, WIDE)], rhs.at[1, half], y_sem.at[half])
 
     def rhs_copy(n, mat):
-        columns = pl.ds(pl.multiple_of(n * 512, 512), 512)
+        columns = pl.ds(pl.multiple_of(n * WIDE, WIDE), WIDE)
         return pltpu.make_async_copy((dg, du)[mat].at[:, columns], rhs.at[n % 2, mat], rhs_sem.at[n % 2, mat])
 
     def tail_copy(mat):
-        return pltpu.make_async_copy((dg, du)[mat].at[:, pl.ds(3072, 128)], rhs_tail.at[mat], tail_sem.at[mat])
+        return pltpu.make_async_copy((dg, du)[mat].at[:, pl.ds(3072, LANES)], rhs_tail.at[mat], tail_sem.at[mat])
 
     PA, PB = buffers(0)[0], buffers(1)[0]
 
@@ -566,16 +647,16 @@
         y_copy(half).start()
 
     def a_copy(half, x):
-        rows = pl.ds(pl.multiple_of((2 * x + parity(half)) * 128, 128), 128)
-        return pltpu.make_async_copy(aT.at[rows], a.at[half, pl.ds(x * 128, 128)], a_sem.at[half, x])
+        rows = pl.ds(pl.multiple_of((2 * x + parity(half)) * LANES, LANES), LANES)
+        return pltpu.make_async_copy(aT.at[rows], a.at[half, pl.ds(x * LANES, LANES)], a_sem.at[half, x])
 
     for half in range(2):
-        for x in range(4):
+        for x in range(WAY):
             a_copy(half, x).start()
     for mat in range(2):
         rhs_copy(0, mat).start()
         tail_copy(mat).start()
-    send_e[:, :, pl.ds(3, 1)] = jnp.zeros((4, 4, 1, 48, 256), BF)
+    send_e[:, :, pl.ds(3, 1)] = jnp.zeros((WAY, WAY, 1, 48, SIDE), BF)
     for half in range(2):
         y_copy(half).wait()
 
@@ -586,14 +667,14 @@
         def _():
             hid_copy(j + 1).start()
 
-        k = j % 4
+        k = j % WAY
         for half in range(2):
             out = dot(hid[j % 2], rhs[1, half])
-            upper = [out[:256, 256 * n : 256 * n + 256].reshape(4, 64, 256) for n in range(2)]
-            lower = [out[256:, 256 * n : 256 * n + 256].reshape(3, 48, 256) for n in range(2)]
+            upper = [out[:SIDE, SIDE * n : SIDE * n + SIDE].reshape(WAY, 64, SIDE) for n in range(2)]
+            lower = [out[SIDE:, SIDE * n : SIDE * n + SIDE].reshape(3, 48, SIDE) for n in range(2)]
             if half == 0:
 
-                @pl.when(j >= 4)
+                @pl.when(j >= WAY)
                 def _():
                     pair_d(k, 0).wait_recv()
                     pair_d(k, 1).wait_recv()
@@ -601,17 +682,17 @@
             for n in range(2):
                 y = 2 * half + n
 
-                @pl.when(j < 4)
+                @pl.when(j < WAY)
                 def _():
                     send_d[k, y] = upper[n].astype(BF)
                     send_e[k, y, pl.ds(0, 3)] = lower[n].astype(BF)
 
-                @pl.when(j >= 4)
+                @pl.when(j >= WAY)
                 def _():
                     PA[k, y] = (PA[k, y].astype(F32) + upper[n]).astype(BF)
                     PB[k, y, pl.ds(0, 3)] = (PB[k, y, pl.ds(0, 3)].astype(F32) + lower[n]).astype(BF)
 
-        @pl.when(j < 4)
+        @pl.when(j < WAY)
         def _():
             pair_d(k, 0).start()
             pair_d(k, 1).start()
@@ -624,14 +705,14 @@
     for mat in range(2):
         rhs_copy(1, mat).start()
     for half in range(2):
-        for x in range(4):
+        for x in range(WAY):
             a_copy(half, x).wait()
 
     def gate_up(P, send, rights, pair, columns):
         for mat in range(2):
-            send[:, pl.ds(2 * mat, 2)] = dot(a[0], rights(mat)).astype(BF).reshape(4, 2, 4, 16, columns)
+            send[:, pl.ds(2 * mat, 2)] = dot(a[0], rights(mat)).astype(BF).reshape(WAY, 2, WAY, TILE, columns)
         pair.start()
-        own = [dot(a[1], rights(mat)).reshape(4, 2, 4, 16, columns) for mat in range(2)]
+        own = [dot(a[1], rights(mat)).reshape(WAY, 2, WAY, TILE, columns) for mat in range(2)]
         pair.wait_recv()
         for mat in range(2):
             part = pl.ds(2 * mat, 2)
@@ -639,7 +720,7 @@
 
     def pair_u(n):
         return pltpu.make_async_remote_copy(
-            src_ref=send_u.at[n % 2], dst_ref=bufs[16].at[n], send_sem=pair_s.at[4 + n, 0], recv_sem=pair_r.at[4 + n, 0],
+            src_ref=send_u.at[n % 2], dst_ref=bufs[TILE].at[n], send_sem=pair_s.at[WAY + n, 0], recv_sem=pair_r.at[WAY + n, 0],
             device_id=partner, device_id_type=MESH)
 
     pair_t = pltpu.make_async_remote_copy(
@@ -654,9 +735,9 @@
         def _():
             pair_u(n - 2).wait_send()
 
-        gate_up(bufs[16].at[n], send_u.at[n % 2], lambda mat: rhs[n % 2, mat], pair_u(n), 512)
-
-        @pl.when(n < 4)
+        gate_up(bufs[TILE].at[n], send_u.at[n % 2], lambda mat: rhs[n % 2, mat], pair_u(n), WIDE)
+
+        @pl.when(n < WAY)
         def _():
             for mat in range(2):
                 rhs_copy(n + 2, mat).start()
@@ -672,18 +753,18 @@
     lax.fori_loop(0, 6, chunk_step, 0)
     for mat in range(2):
         tail_copy(mat).wait()
-    gate_up(buffers(8)[0], send_t, lambda mat: rhs_tail[mat], pair_t, 128)
+    gate_up(buffers(8)[0], send_t, lambda mat: rhs_tail[mat], pair_t, LANES)
     run(6)
 
-    for k in range(4):
+    for k in range(WAY):
         for which in range(2):
             pair_d(k, which).wait_send()
-    for n in (4, 5):
+    for n in (WAY, 5):
         pair_u(n).wait_send()
     pair_t.wait_send()
     for unit in range(len(UNITS)):
-        for stage in range(5):
-            for copy in copies(unit, stage):
+        for step in range(8):
+            for copy in copies(unit, step):
                 copy.wait_send()
         for copy in out_copies(unit):
             copy.wait()
@@ -695,35 +776,35 @@
     for first, count in KINDS:
         tile = UNITS[first][0]
         bufs += [
-            pltpu.VMEM((count, 4, 4, 4) + tile, BF),
-            pltpu.VMEM((count, 3, 4, 4) + tile, BF),
-            pltpu.VMEM((count, 4, 4) + tile, BF),
-            pltpu.VMEM((count, 4, 4) + tile, F32),
-            pltpu.VMEM((count, 3, 4) + tile, BF),
-            pltpu.VMEM((count, 4) + tile, BF),
-            pltpu.VMEM((count, 4) + tile, F32),
-            pltpu.VMEM((count, 5, 4) + tile, BF),
+            pltpu.VMEM((count, WAY, WAY, WAY) + tile, BF),
+            pltpu.VMEM((count, 3, WAY, WAY) + tile, BF),
+            pltpu.VMEM((count, WAY, WAY) + tile, BF),
+            pltpu.VMEM((count, WAY, WAY) + tile, F32),
+            pltpu.VMEM((count, 3, WAY) + tile, BF),
+            pltpu.VMEM((count, WAY) + tile, BF),
+            pltpu.VMEM((count, WAY) + tile, F32),
+            pltpu.VMEM((count, 5, WAY) + tile, BF),
         ]
     return pl.pallas_call(
         gradients_kernel,
         out_shape=(
-            jax.ShapeDtypeStruct((128, FF), BF),
-            jax.ShapeDtypeStruct((128, FF), BF),
-            jax.ShapeDtypeStruct((400, D), BF),
+            jax.ShapeDtypeStruct((LANES, FF), BF),
+            jax.ShapeDtypeStruct((LANES, FF), BF),
+            jax.ShapeDtypeStruct((OWN, D), BF),
         ),
         in_specs=[ANY] * 5,
         out_specs=(ANY,) * 3,
         scratch_shapes=[
-            pltpu.VMEM((2, 512, T), BF),
-            pltpu.VMEM((2, 2, T, 512), BF),
-            pltpu.VMEM((2, T, 128), BF),
-            pltpu.VMEM((2, 400, T), BF),
-            pltpu.VMEM((4, 4, 4, 64, 256), BF),
-            pltpu.VMEM((4, 4, 4, 48, 256), BF),
-            pltpu.VMEM((2, 4, 4, 4, 16, 512), BF),
-            pltpu.VMEM((4, 4, 4, 16, 128), BF),
+            pltpu.VMEM((2, WIDE, T), BF),
+            pltpu.VMEM((2, 2, T, WIDE), BF),
+            pltpu.VMEM((2, T, LANES), BF),
+            pltpu.VMEM((2, OWN, T), BF),
+            pltpu.VMEM((WAY, WAY, WAY, 64, SIDE), BF),
+            pltpu.VMEM((WAY, WAY, WAY, 48, SIDE), BF),
+            pltpu.VMEM((2, WAY, WAY, WAY, TILE, WIDE), BF),
+            pltpu.VMEM((WAY, WAY, WAY, TILE, LANES), BF),
             *bufs,
-            dma((11, 2)), dma((11, 2)), dma((9, 5, 3)), dma((9, 5, 3)), dma((2, 4)), dma((2, 2)), dma((2,)), dma((2,)), dma((2,)), dma((9, 16)),
+            dma((11, 2)), dma((11, 2)), dma((9, 8, 3)), dma((9, 8, 3)), dma((2, WAY)), dma((2, 2)), dma((2,)), dma((2,)), dma((2,)), dma((9, TILE)),
         ],
         compiler_params=pltpu.CompilerParams(collective_id=1 + number, has_side_effects=True, vmem_limit_bytes=VMEM_LIMIT),
         cost_estimate=cost(3, 60_000_000),

time: 572 us -> 577 us (level)
  no operation moved by 1% of the time
where the time goes in v2:
time: 577 us; the launch traced here: 569 us
  Pallas kernels  549 us (95%)
  other arithmetic  18.1 us (3%)
    pallas_call x2, Pallas kernels, gradients(): pl.pallas_call(gradients_kernel, out_shape=(jax.ShapeDtypeStruct((LANES,...  257 us
    pallas_call x1, Pallas kernels, forward(): pl.pallas_call(forward_kernel, out_shape=(jax.ShapeDtypeStruct((2, 8, LAN...  130 us
    pallas_call x2, Pallas kernels, hidden(): pl.pallas_call(functools.partial(hidden_kernel, number, want_hid), grid=(...  119 us
    pallas_call x1, Pallas kernels, input_gradient(): pl.pallas_call(functools.partial(input_kernel, number), grid=(T // TM,),...  42.4 us
    convert_element_type x2, other arithmetic, adamw(): return ((w - 0.02 * step).astype(BF), m, v)  18.1 us

profile of v2, /device:TPU:0, one launch (start us, length us, event | category | flops | bytes accessed | tf_op | source)
XLA Modules:
  0.0 568.6 jit_solution(10417815280506325314)
XLA Ops:
  0.6 130.4 %forward.1 = (bf16[2,8,128,3200]{3,2,1,0:T(8,128)(2,1)}, bf16[2,8,128,3200]{3,2,1,0:T(8,128)(2,1)}, bf16[2,8,400,1024]{3,2,1,0:T(8,128)(2,1)}, bf16[3200,2048]{1...) custom-call(bf16[2048,1024]{1,0:T(8,128)(2,1)} %bitcast.20, bf16[2,128,3200]{2,1,0:T(8,128)(2,1)} %g_hbm.1, ...), custom_call_target="tpu_custom_call" | custom-call | flops 40265318400 | bytes 60000000 | tf_op jit(solution)/shard_map/forward/pallas_call | solution.py:314
  131.0 61.8 %hidden_1.1 = (bf16[3200,2048]{1,0:T(8,128)(2,1)}, bf16[1024,2048]{1,0:T(8,128)(2,1)}, bf16[2048,3200]{1,0:T(8,128)(2,1)}, bf16[2048,3200]{1,0:T(8,128)(2,1)}) custom-call(bf16[2048,1024]{1,0:T(8,128)(2,1)} %get-tuple-element.29.h, bf16[2048,1024]{1,0:T(8,128)(2,1)} %bitcast.17, bf16[2,1024,3200]{2,1,0:T(8,128)(2,1)} %bitcast.22, ...), custom_call_target="tpu_custom_call" | custom-call | flops 40265318400 | bytes 70000000 | tf_op jit(solution)/shard_map/hidden_1/pallas_call | solution.py:398
  192.8 128.3 %gradients_1.1 = (bf16[128,3200]{1,0:T(8,128)(2,1)}, bf16[128,3200]{1,0:T(8,128)(2,1)}, bf16[400,1024]{1,0:T(8,128)(2,1)}) custom-call(bf16[1024,2048]{1,0:T(8,128)(2,1)} %get-tuple-element.38.aT, bf16[3200,2048]{1,0:T(8,128)(2,1)} %get-tuple-element.39.hidT, bf16[2048,3200]{1,0:T(8,128)(2,1)} %get-tuple-element.33.dg, ...), custom_call_target="tpu_custom_call" | custom-call | flops 40265318400 | bytes 60000000 | tf_op jit(solution)/shard_map/gradients_1/pallas_call | solution.py:788
  321.1 42.4 %input_1.1.by_y = bf16[2048,1024]{1,0:T(8,128)(2,1)} custom-call(bf16[2048,1024]{1,0:T(8,128)(2,1)} %get-tuple-element.29.h, bf16[2048,1024]{1,0:T(8,128)(2,1)} %bitcast.19, bf16[2048,3200]{1,0:T(8,128)(2,1)} %get-tuple-element.33.dg, bf16[2048,3200]{1,0:T(8,128)(2,1)} %get-tuple-element.34.du, bf16[2,1024,3200]{2,1,0:T(8,128)(2,1)} %bitcast.23, ...), custom_call_target="tpu_custom_call" | custom-call | flops 26843545600 | bytes 50000000 | tf_op jit(solution)/shard_map/input_1/pallas_call | solution.py:444
  363.6 57.2 %hidden_0.1 = (bf16[2048,3200]{1,0:T(8,128)(2,1)}, bf16[2048,3200]{1,0:T(8,128)(2,1)}) custom-call(bf16[2048,1024]{1,0:T(8,128)(2,1)} %bitcast.21, bf16[2048,1024]{1,0:T(8,128)(2,1)} %input_1.1.by_y, bf16[2,1024,3200]{2,1,0:T(8,128)(2,1)} %bitcast.24, bf16[2,1024,3200]{2,1,0:T(8,128)(2,1)} %bitcast.27, bf16[2,3200,1024]{2,1,0:T(8,128)(2,1)} %bitcast.29), custom_call_target="tpu_custom_call" | custom-call | flops 40265318400 | bytes 70000000 | tf_op jit(solution)/shard_map/hidden_0/pallas_call | solution.py:398
  420.8 0.0 copy-start.4
  420.8 128.4 %gradients_0.1 = (bf16[128,3200]{1,0:T(8,128)(2,1)}, bf16[128,3200]{1,0:T(8,128)(2,1)}, bf16[400,1024]{1,0:T(8,128)(2,1)}) custom-call(bf16[1024,2048]{1,0:T(8,128)(2,1)} %get-tuple-element.27.aT, bf16[3200,2048]{1,0:T(8,128)(2,1)} %get-tuple-element.28.hidT, bf16[2048,3200]{1,0:T(8,128)(2,1)} %get-tuple-element.35.dg, ...), custom_call_target="tpu_custom_call" | custom-call | flops 40265318400 | bytes 60000000 | tf_op jit(solution)/shard_map/gradients_0/pallas_call | solution.py:788
  549.2 0.0 copy-done.4
  549.2 0.0 copy-start
  549.2 0.0 copy-start.1
  549.3 0.0 copy-start.2
  549.3 0.0 copy-start.3
  549.3 0.0 copy-start.5
  549.3 13.9 %fusion.2 = (bf16[2,128,3200]{2,1,0:T(8,128)(2,1)}, f32[2,128,3200]{2,1,0:T(8,128)}, f32[2,128,3200]{2,1,0:T(8,128)}, bf16[2,128,3200]{2,1,0:T(8,128)(2,1)}, f32...) fusion(bf16[2,128,3200]{2,1,0:T(8,128)(2,1)} %g_hbm.1, bf16[1,128,3200]{2,1,0:T(8,128)(2,1)S(1)} %bitcast.12, ...), kind=kLoop, calls=%fused_computation.14 | loop fusion | flops 31129600 | bytes 36044800 | tf_op jit(solution)/shard_map/convert_element_type | solution.py:819
  563.2 0.0 copy-done
  563.2 0.0 copy-done.1
  563.2 0.0 copy-done.2
  563.2 0.1 copy-done.3
  563.2 0.8 copy-done.5
  564.0 4.2 fusion.10
Async XLA Ops:
  420.8 128.4 %copy-start.4 = (bf16[128,3200]{1,0:T(8,128)(2,1)S(1)}, bf16[128,3200]{1,0:T(8,128)(2,1)}, u32[]{:S(2)}) copy-start(bf16[128,3200]{1,0:T(8,128)(2,1)} %get-tuple-element.40) | copy-start | bytes 2457604
  549.2 13.9 %copy-start = (f32[2,400,1024]{2,1,0:T(8,128)S(1)}, f32[2,400,1024]{2,1,0:T(8,128)}, u32[]{:S(2)}) copy-start(f32[2,400,1024]{2,1,0:T(8,128)} %param.21) | copy-start | bytes 9830404
  549.2 13.9 %copy-start.1 = (f32[2,400,1024]{2,1,0:T(8,128)S(1)}, f32[2,400,1024]{2,1,0:T(8,128)}, u32[]{:S(2)}) copy-start(f32[2,400,1024]{2,1,0:T(8,128)} %param.18) | copy-start | bytes 9830404
  549.3 13.9 %copy-start.2 = (bf16[2,400,1024]{2,1,0:T(8,128)(2,1)S(1)}, bf16[2,400,1024]{2,1,0:T(8,128)(2,1)}, u32[]{:S(2)}) copy-start(bf16[2,400,1024]{2,1,0:T(8,128)(2,1)} %d_hbm.1) | copy-start | bytes 4915204
  549.3 14.0 %copy-start.3 = (bf16[400,1024]{1,0:T(8,128)(2,1)S(1)}, bf16[400,1024]{1,0:T(8,128)(2,1)}, u32[]{:S(2)}) copy-start(bf16[400,1024]{1,0:T(8,128)(2,1)} %get-tuple-element.44) | copy-start | bytes 2457604
  549.3 14.7 %copy-start.5 = (bf16[400,1024]{1,0:T(8,128)(2,1)S(1)}, bf16[400,1024]{1,0:T(8,128)(2,1)}, u32[]{:S(2)}) copy-start(bf16[400,1024]{1,0:T(8,128)(2,1)} %get-tuple-element.43) | copy-start | bytes 2457604

commit v3 on v2

--- a/solution.py
+++ b/solution.py
@@ -9,7 +9,7 @@
 
 BF, F32 = jnp.bfloat16, jnp.float32
 MESH = pl.DeviceIdType.MESH
-VMEM_LIMIT = 66_000_000
+VMEM_LIMIT = 67_043_328
 T, D, FF = 2048, 1024, 3200
 WAY = 4
 OWN = 400
@@ -18,6 +18,7 @@
 CHUNKS = tuple((WIDE * j, WIDE) for j in range(6)) + ((3072, LANES),)
 GROUPS = ((0, 1024), (1024, 2176))
 ANY = pl.BlockSpec(memory_space=pl.ANY)
+SIDES, NEAR_FIRST = (1, 3), (1, 3, 2)
 
 
 def dot(a, b):
@@ -64,7 +65,7 @@
     partner = {"r": r, "s": s + 1 - 2 * core}
 
     barrier = pltpu.get_barrier_semaphore()
-    for to in [at(k) for at in (at_x, at_y, at_z) for k in (1, 2, 3)] + [partner]:
+    for to in [at(k) for at in (at_x, at_y, at_z) for k in NEAR_FIRST] + [partner]:
         pl.semaphore_signal(barrier, inc=1, device_id=to, device_id_type=MESH)
     pl.semaphore_wait(barrier, 10)
 
@@ -80,14 +81,6 @@
             return whole.at[l, b]
         p = piece(rows, half, j)
         return whole.at[l, b, p[0], p[1]]
-
-    def halved(ref, rows, back):
-        if rows == LANES:
-            return ref.at[:, pl.ds(1664 * back, 1664 - LANES * back)]
-        return ref.at[pl.ds(208 * back, 208 - TILE * back), :]
-
-    def source(k):
-        return 2 * ((cx + WAY - k) % WAY) + core
 
     def c1(i, half, k):
         shard, l, whole, _, rows = mats[i]
@@ -95,32 +88,19 @@
         p = piece(rows, half, j)
         return pltpu.make_async_remote_copy(
             src_ref=shard.at[l, p[0], p[1]], dst_ref=block(whole, l, s, rows, half, j),
-            send_sem=s1.at[i, half, k // 2], recv_sem=r1.at[i, half, k // 2], device_id=at_x(k), device_id_type=MESH)
-
-    def f1(i, half, k):
-        _, l, whole, _, rows = mats[i]
-        ref = halved(block(whole, l, source(k), rows, half, (y, z)[half]), rows, k // 2)
-        return pltpu.make_async_remote_copy(
-            src_ref=ref, dst_ref=ref, send_sem=s1.at[i, half, 2 + k // 2], recv_sem=r1.at[i, half, 2 + k // 2],
-            device_id=at_x(k), device_id_type=MESH)
+            send_sem=s1.at[i, half, k - 1], recv_sem=r1.at[i, half, k - 1], device_id=at_x(k), device_id_type=MESH)
 
     def c2(i, half, k, q):
         _, l, whole, _, rows = mats[i]
-        ref = block(whole, l, source(k), rows, half, (y, z)[half])
+        b = 2 * ((cx + WAY - k) % WAY) + core
+        ref = block(whole, l, b, rows, half, (y, z)[half])
         return pltpu.make_async_remote_copy(
-            src_ref=ref, dst_ref=ref, send_sem=s2.at[i, half, k - 1, q // 2], recv_sem=r2.at[i, half, k - 1, q // 2],
-            device_id=(at_y, at_z)[half](q), device_id_type=MESH)
-
-    def f2(i, half, k, q):
-        _, l, whole, _, rows = mats[i]
-        ref = halved(block(whole, l, source(k), rows, half, ((y, z)[half] + WAY - q) % WAY), rows, q // 2)
-        return pltpu.make_async_remote_copy(
-            src_ref=ref, dst_ref=ref, send_sem=s2.at[i, half, k - 1, 2 + q // 2], recv_sem=r2.at[i, half, k - 1, 2 + q // 2],
+            src_ref=ref, dst_ref=ref, send_sem=s2.at[i, half, k - 1, q - 1], recv_sem=r2.at[i, half, k - 1, q - 1],
             device_id=(at_y, at_z)[half](q), device_id_type=MESH)
 
     def c3(i, k):
         shard, l, whole, _, rows = mats[i]
-        b = source(k)
+        b = 2 * ((cx + WAY - k) % WAY) + core
         src = shard.at[l] if k == 0 else whole.at[l, b]
         return pltpu.make_async_remote_copy(
             src_ref=src, dst_ref=whole.at[l, b], send_sem=s3.at[i, k], recv_sem=r3.at[i, k], device_id=partner, device_id_type=MESH)
@@ -133,45 +113,26 @@
         _, l, whole, stage, _ = mats[i]
         return pltpu.make_async_copy(stage.at[l], whole.at[l, s], own_sem.at[i])
 
-    sides, halves = (1, 3), range(2)
+    near_first = NEAR_FIRST
 
     def p1(i):
-        for k in sides:
-            for half in halves:
+        for k in near_first:
+            for half in range(2):
                 c1(i, half, k).start()
         c3(i, 0).start()
 
     def p2(i):
-        for k in sides:
-            for half in halves:
+        for k in near_first:
+            for half in range(2):
                 c1(i, half, k).wait_recv()
-                f1(i, half, k).start()
-                for q in sides:
+                for q in near_first:
                     c2(i, half, k, q).start()
 
-    def p2b(i):
-        for half in halves:
-            for k in sides:
-                f1(i, half, k).wait_recv()
-            for q in sides:
-                c2(i, half, 2, q).start()
-        for k in sides:
-            for half in halves:
-                for q in sides:
+    def p3(i):
+        for k in near_first:
+            for half in range(2):
+                for q in near_first:
                     c2(i, half, k, q).wait_recv()
-                    f2(i, half, k, q).start()
-
-    def p2c(i):
-        for half in halves:
-            for q in sides:
-                c2(i, half, 2, q).wait_recv()
-                f2(i, half, 2, q).start()
-
-    def p3(i):
-        for k in (1, 3, 2):
-            for half in halves:
-                for q in sides:
-                    f2(i, half, k, q).wait_recv()
             c3(i, k).start()
 
     def arrived(i):
@@ -205,17 +166,11 @@
         stage_out(i).start()
     p2(0)
     p2(1)
-    p2b(0)
-    p2c(0)
+    p3(0)
     p2(2)
-    p2b(1)
-    p3(0)
-    p2c(1)
     p2(3)
     load_start(0)
-    p2b(2)
     p3(1)
-    p2c(2)
     p2(WAY)
     load_start(1)
     x_copy.wait()
@@ -256,26 +211,16 @@
         @pl.when(m == 0)
         def _():
             p2(5)
-            p2b(3)
             p3(2)
-            p2c(3)
-            p2b(WAY)
 
         @pl.when(m == 1)
         def _():
             p3(3)
             load_start(2)
-            p2c(WAY)
-            p2b(5)
 
         @pl.when(m == 2)
         def _():
             p3(WAY)
-            p2c(5)
-
-        @pl.when(m == 3)
-        def _():
-            p3(5)
 
         return carry
 
@@ -283,6 +228,11 @@
         out = dot(hid[rows_of(m), :], wd[...]).astype(BF)
         x[rows_of(m), :] = (x[rows_of(m), :].astype(F32) + out.astype(F32)).astype(BF)
         h_copy(m).start()
+
+        @pl.when(m == 1)
+        def _():
+            p3(5)
+
         return carry
 
     lax.fori_loop(0, WAY, up_step, 0)
@@ -293,14 +243,11 @@
         if i > 2:
             arrived(i)
             stage_out(i).wait()
-        for half in halves:
-            for k in sides:
+        for k in NEAR_FIRST:
+            for half in range(2):
                 c1(i, half, k).wait_send()
-                f1(i, half, k).wait_send()
-            for k in (1, 2, 3):
-                for q in sides:
+                for q in NEAR_FIRST:
                     c2(i, half, k, q).wait_send()
-                    f2(i, half, k, q).wait_send()
         for k in range(WAY):
             c3(i, k).wait_send()
     hid_copy(3).wait()
@@ -335,8 +282,8 @@
             pltpu.VMEM((TM, D), BF),
             pltpu.VMEM((D, TM), BF),
             pltpu.VMEM((FF, TM), BF),
-            dma((6, 2, WAY)), dma((6, 2, WAY)), dma((6, 2, 3, WAY)), dma((6, 2, 3, WAY)), dma((6, WAY)), dma((6, WAY)),
-            dma((6,)), dma((6,)), dma, dma((3, 8)), dma((WAY,)), dma((WAY,)), dma((WAY,)),
+            *[dma((6, 2, 3))] * 2, *[dma((6, 2, 3, 3))] * 2, *[dma((6, WAY))] * 2,
+            dma((6,)), dma((6,)), dma, dma((3, 8)), *[dma((WAY,))] * 3,
         ],
         compiler_params=pltpu.CompilerParams(collective_id=0, has_side_effects=True, vmem_limit_bytes=VMEM_LIMIT),
         cost_estimate=cost(3, 60_000_000),
@@ -408,50 +355,10 @@
             pltpu.VMEM((FF, D), BF),
             pltpu.SemaphoreType.DMA((3, len(GROUPS))),
         ],
-        compiler_params=pltpu.CompilerParams(vmem_limit_bytes=VMEM_LIMIT, dimension_semantics=("arbitrary",)),
+        compiler_params=pltpu.CompilerParams(vmem_limit_bytes=VMEM_LIMIT),
         cost_estimate=cost(3, 70_000_000),
         name=f"hidden_{number}",
     )(h, by_y, G.reshape(2, D, FF), U.reshape(2, D, FF), Dn.reshape(2, FF, D))
-
-
-def input_kernel(number, h, by_y, dg, du, G, U, out, wg, wu, sems):
-    m = pl.program_id(0)
-    copies = [pltpu.make_async_copy(W.at[number], w, sems.at[i]) for i, (W, w) in enumerate(((G, wg), (U, wu)))]
-
-    @pl.when(m == 0)
-    def _():
-        copies[0].start()
-        copies[1].start()
-        copies[0].wait()
-
-    by_a = dot_bt(dg[...], wg[...]).astype(BF).astype(F32)
-
-    @pl.when(m == 0)
-    def _():
-        copies[1].wait()
-
-    by_a = (by_a + dot_bt(du[...], wu[...]).astype(BF).astype(F32)).astype(BF).astype(F32)
-    wide = h[...].astype(F32)
-    scale = lax.rsqrt(jnp.mean(wide * wide, -1, keepdims=True) + 1e-6)
-    along = jnp.mean(by_a * wide, -1, keepdims=True)
-    by_h = (by_a * scale - wide * (scale * scale * scale * along)).astype(BF)
-    out[...] = (by_y[...].astype(F32) + by_h.astype(F32)).astype(BF)
-
-
-def input_gradient(number, h, by_y, dg, du, G, U):
-    tile = pl.BlockSpec((TM, D), lambda m: (m, 0))
-    wide = pl.BlockSpec((TM, FF), lambda m: (m, 0))
-    return pl.pallas_call(
-        functools.partial(input_kernel, number),
-        grid=(T // TM,),
-        out_shape=jax.ShapeDtypeStruct((T, D), BF),
-        in_specs=[tile, tile, wide, wide, ANY, ANY],
-        out_specs=tile,
-        scratch_shapes=[pltpu.VMEM((D, FF), BF), pltpu.VMEM((D, FF), BF), pltpu.SemaphoreType.DMA((2,))],
-        compiler_params=pltpu.CompilerParams(vmem_limit_bytes=VMEM_LIMIT, dimension_semantics=("arbitrary",)),
-        cost_estimate=cost(2, 50_000_000),
-        name=f"input_{number}",
-    )(h, by_y, dg, du, G.reshape(2, D, FF), U.reshape(2, D, FF))
 
 
 UNITS = (
@@ -465,16 +372,18 @@
     ((TILE, WIDE), "zxy", "yz"),
     ((TILE, LANES), "xyz", "yz"),
 )
-SIDES, NEAR_FIRST = (1, 3), (1, 3, 2)
 KINDS = ((0, 1), (1, 1), (2, 6), (8, 1))
 
 
-def gradients_kernel(
-    aT, hidT, dg, du, by_y, g_out, u_out, d_out,
-    a, rhs, rhs_tail, hid, send_d, send_e, send_u, send_t,
-    *rest,
-):
-    bufs, (pair_s, pair_r, s, r, a_sem, rhs_sem, tail_sem, hid_sem, y_sem, out_sem) = rest[:32], rest[32:]
+def gradients_kernel(number, aT, hidT, by_y, h, G, U, Dn, *rest):
+    if number:
+        dg, du, g_out, u_out, d_out, h_out = rest[:6]
+        rest = rest[6:]
+    else:
+        g_out, u_out, d_out = rest[:3]
+        rest = rest[3:]
+    a, rhs, hid, send_d, send_e, send_u, send_t, wg, wu, *rest = rest
+    bufs, (pair_s, pair_r, s, r, a_sem, rhs_sem, hid_sem, y_sem, out_sem, w_sem, more, own, *wd) = rest[:24], rest[24:]
     ri, si = lax.axis_index("r"), lax.axis_index("s")
     core = si % 2
     me = {"x": si // 2, "y": ri // WAY, "z": ri % WAY}
@@ -488,14 +397,14 @@
 
     partner = {"r": ri, "s": si + 1 - 2 * core}
     barrier = pltpu.get_barrier_semaphore()
-    for to in [peer(axis, k) for axis in "xyz" for k in (1, 2, 3)] + [partner]:
+    for to in [peer(axis, k) for axis in "xyz" for k in NEAR_FIRST] + [partner]:
         pl.semaphore_signal(barrier, inc=1, device_id=to, device_id_type=MESH)
     pl.semaphore_wait(barrier, 10)
 
     def buffers(unit):
         for kind, (first, count) in enumerate(KINDS):
             if first <= unit < first + count:
-                return [ref.at[unit - first] for ref in bufs[8 * kind : 8 * kind + 8]]
+                return [ref.at[unit - first] for ref in bufs[6 * kind : 6 * kind + 6]]
 
     def others(unit, stage):
         order = UNITS[unit][1]
@@ -520,7 +429,7 @@
         return RA.at[pl.ds(1, WAY) if half is None else pl.ds(1 + 2 * half, 2), index]
 
     def copies(unit, step):
-        P, R1, Q1, F1, R2, Q2, F2, RA = buffers(unit)
+        P, R1, Q1, R2, Q2, RA = buffers(unit)
         order, gather = UNITS[unit][1:]
         made = []
         for k in NEAR_FIRST if step in (WAY, 5) else SIDES:
@@ -558,7 +467,7 @@
             copy.wait_recv()
 
     def out_copies(unit):
-        RA = buffers(unit)[7]
+        RA = buffers(unit)[5]
         made = []
         if unit < 2:
             base, rows = SIDE * unit, UNITS[unit][0][0]
@@ -573,24 +482,34 @@
         return [pltpu.make_async_copy(src, dst, out_sem.at[unit, n]) for n, (src, dst) in enumerate(made)]
 
     def advance(unit, step):
-        P, R1, Q1, F1, R2, Q2, F2, RA = buffers(unit)
+        P, R1, Q1, R2, Q2, RA = buffers(unit)
         wait(unit, step)
         stage = step // 2
+        order = UNITS[unit][1]
+
+        def first(index):
+            at = list(index)
+            at.insert("xyz".index(order[0]), me[order[0]])
+            return P[tuple(at)].astype(F32) + R1[(0, *index)].astype(F32) + R1[(1, *index)].astype(F32)
+
         if step in (0, 2):
-            axis, R, own, to = UNITS[unit][1][stage], (R1, R2)[stage], (P, F1)[stage], (P, Q1)[stage]
+            R, to = (R1, R2)[stage], (P, Q1)[stage]
             for k in SIDES:
-                index = cut(unit, stage, (me[axis] + k) % WAY, k // 2)
-                to[index] = (own[index].astype(F32) + R[2, pl.ds(2 * (k // 2), 2)].astype(F32)).astype(BF)
-        elif step in (1, 3):
-            R, own, F, Q = (R1, R2)[stage], (P, F1)[stage], (F1, F2)[stage], (Q1, Q2)[stage]
-            mine = own[cut(unit, stage, me[UNITS[unit][1][stage]])].astype(F32)
-            mine += R[0].astype(F32) + R[1].astype(F32)
-            F[...], Q[...] = mine, mine.astype(BF)
-        elif step == WAY:
-            mine = F2[me[UNITS[unit][1][2]]]
-            for k in range(3):
-                mine += RA[0, k].astype(F32)
-            RA[1 + me["y"], me["z"]] = mine.astype(BF)
+                index = cut(unit, stage, (me[order[stage]] + k) % WAY, k // 2)
+                own = first(index) if stage else P[index].astype(F32)
+                to[index] = (own + R[2, pl.ds(2 * (k // 2), 2)].astype(F32)).astype(BF)
+        elif step == 1:
+            Q1[...] = first((slice(None), slice(None))).astype(BF)
+        elif step in (3, WAY):
+            every = slice(None) if step == 3 else me[order[2]]
+            index = [every if axis == order[2] else me[axis] for axis in others(unit, 1)]
+            mine = first(tuple(index)) + R2[0, every].astype(F32) + R2[1, every].astype(F32)
+            if step == 3:
+                Q2[...] = mine.astype(BF)
+            else:
+                for k in range(3):
+                    mine += RA[0, k].astype(F32)
+                RA[1 + me["y"], me["z"]] = mine.astype(BF)
         if step < 7:
             start(unit, step + 1)
         else:
@@ -598,23 +517,18 @@
                 copy.start()
 
     after = (
-        ("cs",),
-        ("dsb0a0c0",),
-        ("esb1d0",),
-        ("fsa1b2c1e0",),
-        ("gsb3a2c2d1f0",),
-        ("hsb4a3c3d2e1g0h0",),
-        ("isb5a4c4d3e2f1i0", "b6a5c5d4e3f2b7a6c6d5e4f3a7c7", "d6e5f4g1h1i1d7e6f5g2h2i2e7f6", "g3h3i3f7g4h4i4g5h5i5g6h6i6g7h7i7"),
+        "a0b0", "cs", "b1c0", "dsa1b2", "a2b3c1d0", "esa3b4c2", "a4b5c3d1e0", "fsa5b6c4d2",
+        "a6b7c5d3e1f0", "gsa7c6d4e2", "c7d5e3f1g0", "hsd6e4f2", "isd7e5f3g1h0", "e6f4g2i0e7f5g3h1i1f6g4h2i2f7g5h3i3g6h4i4g7h5i5h6i6h7i7",
     )
 
     def run(tick):
-        for what in after[tick]:
-            for letter, step in zip(what[::2], what[1::2], strict=True):
-                unit = ord(letter) - ord("a")
-                if step == "s":
-                    start(unit, 0)
-                else:
-                    advance(unit, int(step))
+        what = after[tick]
+        for letter, step in zip(what[::2], what[1::2]):
+            unit = ord(letter) - ord("a")
+            if step == "s":
+                start(unit, 0)
+            else:
+                advance(unit, int(step))
 
     def parity(half):
         return core if half else 1 - core
@@ -627,19 +541,37 @@
     def y_copy(half):
         return pltpu.make_async_copy(by_y.at[:, pl.ds(half * WIDE, WIDE)], rhs.at[1, half], y_sem.at[half])
 
-    def rhs_copy(n, mat):
-        columns = pl.ds(pl.multiple_of(n * WIDE, WIDE), WIDE)
-        return pltpu.make_async_copy((dg, du)[mat].at[:, columns], rhs.at[n % 2, mat], rhs_sem.at[n % 2, mat])
-
-    def tail_copy(mat):
-        return pltpu.make_async_copy((dg, du)[mat].at[:, pl.ds(3072, LANES)], rhs_tail.at[mat], tail_sem.at[mat])
+    def columns_of(n):
+        if isinstance(n, int) and n == 6:
+            return pl.ds(3072, LANES), pl.ds(0, LANES)
+        return pl.ds(pl.multiple_of(n * WIDE, WIDE), WIDE), slice(None)
+
+    def w_copies(n):
+        columns, to = columns_of(n)
+        made = [(W.at[number, :, columns], w.at[n % 2, :, to]) for W, w in ((G, wg), (U, wu))]
+        if number:
+            made += [(d.at[:, columns], rhs.at[n % 2, mat, :, to]) for mat, d in enumerate((dg, du))]
+        else:
+            made.append((Dn.at[number, columns, :], wd[0].at[n % 2, to, :]))
+        return [pltpu.make_async_copy(src, dst, w_sem.at[n % 2, i]) for i, (src, dst) in enumerate(made)]
+
+    def w_start(n):
+        for copy in w_copies(n):
+            copy.start()
+
+    def w_wait(n):
+        for copy in w_copies(n):
+            copy.wait()
+
+    def tile(t):
+        return pl.ds(pl.multiple_of(t * TM, TM), TM)
 
     PA, PB = buffers(0)[0], buffers(1)[0]
 
     def pair_d(k, which):
         src, dst = ((send_d, PA), (send_e, PB))[which]
         return pltpu.make_async_remote_copy(
-            src_ref=src.at[k], dst_ref=dst.at[k], send_sem=pair_s.at[k, which], recv_sem=pair_r.at[k, which],
+            src_ref=src.at[k % 2], dst_ref=dst.at[k], send_sem=pair_s.at[k, which], recv_sem=pair_r.at[k, which],
             device_id=partner, device_id_type=MESH)
 
     hid_copy(0).start()
@@ -653,10 +585,13 @@
     for half in range(2):
         for x in range(WAY):
             a_copy(half, x).start()
-    for mat in range(2):
-        rhs_copy(0, mat).start()
-        tail_copy(mat).start()
-    send_e[:, :, pl.ds(3, 1)] = jnp.zeros((WAY, WAY, 1, 48, SIDE), BF)
+    w_start(0)
+    if number:
+        more[...] = jnp.zeros_like(more)
+    else:
+        x_copy = pltpu.make_async_copy(h, more, rhs_sem)
+        x_copy.start()
+    send_e[:, :, pl.ds(3, 1)] = jnp.zeros((2, WAY, 1, 48, SIDE), BF)
     for half in range(2):
         y_copy(half).wait()
 
@@ -668,6 +603,12 @@
             hid_copy(j + 1).start()
 
         k = j % WAY
+
+        @pl.when((j == 2) | (j == 3))
+        def _():
+            pair_d(k - 2, 0).wait_send()
+            pair_d(k - 2, 1).wait_send()
+
         for half in range(2):
             out = dot(hid[j % 2], rhs[1, half])
             upper = [out[:SIDE, SIDE * n : SIDE * n + SIDE].reshape(WAY, 64, SIDE) for n in range(2)]
@@ -684,8 +625,8 @@
 
                 @pl.when(j < WAY)
                 def _():
-                    send_d[k, y] = upper[n].astype(BF)
-                    send_e[k, y, pl.ds(0, 3)] = lower[n].astype(BF)
+                    send_d[k % 2, y] = upper[n].astype(BF)
+                    send_e[k % 2, y, pl.ds(0, 3)] = lower[n].astype(BF)
 
                 @pl.when(j >= WAY)
                 def _():
@@ -702,25 +643,75 @@
     lax.fori_loop(0, 8, down_step, 0)
     for unit in range(2):
         start(unit, 0)
-    for mat in range(2):
-        rhs_copy(1, mat).start()
     for half in range(2):
         for x in range(WAY):
             a_copy(half, x).wait()
 
-    def gate_up(P, send, rights, pair, columns):
+    def by_gate_up(n, size):
+        w_wait(n)
+        if not (isinstance(n, int) and n == 6):
+
+            @pl.when(n < 5)
+            def _():
+                w_start(n + 1)
+
+            @pl.when(n == 5)
+            def _():
+                w_start(6)
+
+        def one(t, carry):
+            part = pl.ds(0, size)
+            gate, up = (dot(more[tile(t), :], w[n % 2, :, part]) for w in (wg, wu))
+            down = wd[0].at[n % 2, part]
+            by_hid = dot_bt(rhs[1, 0, tile(t), :], down[:, :WIDE]) + dot_bt(rhs[1, 1, tile(t), :], down[:, WIDE:])
+            by_hid = by_hid.astype(BF).astype(F32)
+            sig = jax.nn.sigmoid(gate)
+            act = gate * sig
+            rhs[0, 1, tile(t), part] = (by_hid * act).astype(BF)
+            rhs[0, 0, tile(t), part] = (by_hid * up * (sig + act * (1.0 - sig))).astype(BF)
+            return carry
+
+        lax.fori_loop(0, T // TM, one, 0)
+
+    def by_input(n, size):
+        part = pl.ds(0, size)
+
+        def one(t, carry):
+            for half in range(2):
+                to = pl.ds(WIDE * half, WIDE)
+                gate, up = (dot_bt(rhs[n % 2, mat, tile(t), part], w[n % 2, to, part]) for mat, w in enumerate((wg, wu)))
+                more[tile(t), to] += gate + up
+            return carry
+
+        lax.fori_loop(0, T // TM, one, 0)
+
+    if number:
+        w_start(1)
+    else:
+        x_copy.wait()
+
+        def norm(t, carry):
+            more[tile(t), :] = normed(more[tile(t), :])
+            return carry
+
+        lax.fori_loop(0, T // TM, norm, 0)
+        by_gate_up(0, WIDE)
+
+    def gate_up(send, rights, pair, kept, columns):
         for mat in range(2):
             send[:, pl.ds(2 * mat, 2)] = dot(a[0], rights(mat)).astype(BF).reshape(WAY, 2, WAY, TILE, columns)
         pair.start()
-        own = [dot(a[1], rights(mat)).reshape(WAY, 2, WAY, TILE, columns) for mat in range(2)]
+        for mat in range(2):
+            kept[:, pl.ds(2 * mat, 2)] = dot(a[1], rights(mat)).reshape(WAY, 2, WAY, TILE, columns)
+
+    def pair_sum(P, pair, kept):
         pair.wait_recv()
-        for mat in range(2):
-            part = pl.ds(2 * mat, 2)
-            P[:, part] = (P[:, part].astype(F32) + own[mat]).astype(BF)
+        for x in range(WAY):
+            P[x] = (P[x].astype(F32) + kept[x]).astype(BF)
 
     def pair_u(n):
         return pltpu.make_async_remote_copy(
-            src_ref=send_u.at[n % 2], dst_ref=bufs[TILE].at[n], send_sem=pair_s.at[WAY + n, 0], recv_sem=pair_r.at[WAY + n, 0],
+            src_ref=send_u.at[n % 2], dst_ref=bufs[12].at[n], send_sem=pair_s.at[WAY + n, 0], recv_sem=pair_r.at[WAY + n, 0],
             device_id=partner, device_id_type=MESH)
 
     pair_t = pltpu.make_async_remote_copy(
@@ -728,35 +719,94 @@
         device_id=partner, device_id_type=MESH)
 
     def chunk_step(n, carry):
-        for mat in range(2):
-            rhs_copy(n, mat).wait()
+        if number:
+            w_wait(n)
 
         @pl.when(n >= 2)
         def _():
             pair_u(n - 2).wait_send()
 
-        gate_up(bufs[TILE].at[n], send_u.at[n % 2], lambda mat: rhs[n % 2, mat], pair_u(n), WIDE)
-
-        @pl.when(n < WAY)
-        def _():
-            for mat in range(2):
-                rhs_copy(n + 2, mat).start()
-
-        for tick in range(6):
-
-            @pl.when(n == tick)
+        slot = n % 2 if number else 0
+        gate_up(send_u.at[n % 2], lambda mat: rhs[slot, mat], pair_u(n), own, WIDE)
+        for now in range(6):
+
+            @pl.when(n == now)
             def _():
-                run(tick)
+                run(2 * now)
+
+        if number:
+            by_input(n, WIDE)
+
+            @pl.when(n < WAY)
+            def _():
+                w_start(n + 2)
+
+            @pl.when(n == WAY)
+            def _():
+                w_start(6)
+
+        else:
+
+            @pl.when(n < 5)
+            def _():
+                by_gate_up(n + 1, WIDE)
+
+            @pl.when(n == 5)
+            def _():
+                by_gate_up(6, LANES)
+
+        pair_sum(bufs[12].at[n], pair_u(n), own)
+        for now in range(6):
+
+            @pl.when(n == now)
+            def _():
+                run(2 * now + 1)
 
         return carry
 
     lax.fori_loop(0, 6, chunk_step, 0)
-    for mat in range(2):
-        tail_copy(mat).wait()
-    gate_up(buffers(8)[0], send_t, lambda mat: rhs_tail[mat], pair_t, LANES)
-    run(6)
-
-    for k in range(WAY):
+    if number:
+        w_wait(6)
+    kept = own.at[:, :, :, :, pl.ds(0, LANES)]
+    gate_up(send_t, lambda mat: rhs[0, mat, :, pl.ds(0, LANES)], pair_t, kept, LANES)
+    pair_sum(buffers(8)[0], pair_t, kept)
+    run(12)
+    if number:
+        by_input(6, LANES)
+
+        def part_copies(slot, whole, back=False):
+            made = []
+            for half in range(2):
+                refs = whole.at[:, pl.ds(half * WIDE, WIDE)], rhs.at[slot, half]
+                made.append(pltpu.make_async_copy(*(refs[::-1] if back else refs), y_sem.at[half] if slot else rhs_sem.at[half]))
+            return made
+
+        loads = part_copies(0, h) + part_copies(1, by_y)
+        for copy in loads:
+            copy.start()
+        for copy in loads:
+            copy.wait()
+
+        def one(t, carry):
+            by_a = more[tile(t), :].astype(BF).astype(F32)
+            by_a = [by_a[:, :WIDE], by_a[:, WIDE:]]
+            wide = [rhs[0, half, tile(t), :].astype(F32) for half in range(2)]
+            scale = lax.rsqrt(sum(jnp.sum(w * w, -1, keepdims=True) for w in wide) / D + 1e-6)
+            along = sum(jnp.sum(b * w, -1, keepdims=True) for b, w in zip(by_a, wide)) / D
+            for half in range(2):
+                by_h = (by_a[half] * scale - wide[half] * (scale * scale * scale * along)).astype(BF)
+                rhs[0, half, tile(t), :] = (rhs[1, half, tile(t), :].astype(F32) + by_h.astype(F32)).astype(BF)
+            return carry
+
+        lax.fori_loop(0, T // TM, one, 0)
+        stores = part_copies(0, h_out, back=True)
+        for copy in stores:
+            copy.start()
+        for copy in stores:
+            copy.wait()
+    run(13)
+
+    for k in (2, 3):
         for which in range(2):
             pair_d(k, which).wait_send()
     for n in (WAY, 5):
@@ -770,46 +820,39 @@
             copy.wait()
 
 
-def gradients(number, aT, hidT, dg, du, by_y):
+def gradients(number, aT, hidT, by_y, h, G, U, Dn, *by_gate_up):
     dma = pltpu.SemaphoreType.DMA
     bufs = []
     for first, count in KINDS:
-        tile = UNITS[first][0]
-        bufs += [
-            pltpu.VMEM((count, WAY, WAY, WAY) + tile, BF),
-            pltpu.VMEM((count, 3, WAY, WAY) + tile, BF),
-            pltpu.VMEM((count, WAY, WAY) + tile, BF),
-            pltpu.VMEM((count, WAY, WAY) + tile, F32),
-            pltpu.VMEM((count, 3, WAY) + tile, BF),
-            pltpu.VMEM((count, WAY) + tile, BF),
-            pltpu.VMEM((count, WAY) + tile, F32),
-            pltpu.VMEM((count, 5, WAY) + tile, BF),
-        ]
+        shape = UNITS[first][0]
+        for ways in ((WAY, WAY, WAY), (3, WAY, WAY), (WAY, WAY), (3, WAY), (WAY,), (5, WAY)):
+            bufs.append(pltpu.VMEM((count, *ways, *shape), BF))
+    outs = [(LANES, FF), (LANES, FF), (OWN, D)] + [(T, D)] * number
     return pl.pallas_call(
-        gradients_kernel,
-        out_shape=(
-            jax.ShapeDtypeStruct((LANES, FF), BF),
-            jax.ShapeDtypeStruct((LANES, FF), BF),
-            jax.ShapeDtypeStruct((OWN, D), BF),
-        ),
-        in_specs=[ANY] * 5,
-        out_specs=(ANY,) * 3,
+        functools.partial(gradients_kernel, number),
+        out_shape=[jax.ShapeDtypeStruct(shape, BF) for shape in outs],
+        in_specs=[ANY] * (9 if number else 7),
+        out_specs=[ANY] * len(outs),
         scratch_shapes=[
             pltpu.VMEM((2, WIDE, T), BF),
             pltpu.VMEM((2, 2, T, WIDE), BF),
-            pltpu.VMEM((2, T, LANES), BF),
             pltpu.VMEM((2, OWN, T), BF),
-            pltpu.VMEM((WAY, WAY, WAY, 64, SIDE), BF),
-            pltpu.VMEM((WAY, WAY, WAY, 48, SIDE), BF),
+            pltpu.VMEM((2, WAY, WAY, 64, SIDE), BF),
+            pltpu.VMEM((2, WAY, WAY, 48, SIDE), BF),
             pltpu.VMEM((2, WAY, WAY, WAY, TILE, WIDE), BF),
             pltpu.VMEM((WAY, WAY, WAY, TILE, LANES), BF),
+            pltpu.VMEM((2, D, WIDE), BF),
+            pltpu.VMEM((2, D, WIDE), BF),
             *bufs,
-            dma((11, 2)), dma((11, 2)), dma((9, 8, 3)), dma((9, 8, 3)), dma((2, WAY)), dma((2, 2)), dma((2,)), dma((2,)), dma((2,)), dma((9, TILE)),
+            *[dma((11, 2))] * 2, *[dma((9, 8, 3))] * 2, dma((2, WAY)), dma((2,)) if number else dma,
+            dma((2,)), dma((2,)), dma((9, TILE)), dma((2, WAY)), pltpu.VMEM((T, D), F32 if number else BF),
+            pltpu.VMEM((WAY, WAY, WAY, TILE, WIDE), F32),
+            *([] if number else [pltpu.VMEM((2, WIDE, D), BF)]),
         ],
         compiler_params=pltpu.CompilerParams(collective_id=1 + number, has_side_effects=True, vmem_limit_bytes=VMEM_LIMIT),
-        cost_estimate=cost(3, 60_000_000),
+        cost_estimate=cost(5 if number else 6, 60_000_000),
         name=f"gradients_{number}",
-    )(aT, hidT, dg, du, by_y)
+    )(aT, hidT, by_y, h, G.reshape(2, D, FF), U.reshape(2, D, FF), Dn.reshape(2, FF, D), *by_gate_up)
 
 
 def adamw(w, m, v, g):
@@ -825,19 +868,17 @@
         x, dy = x[0], dy[0]
         G, U, Dn, hid0, a0, h1 = forward(x, *weights)
         hid1, a1, dg1, du1 = hidden(1, True, h1, dy, G, U, Dn)
-        one = gradients(1, a1, hid1, dg1, du1, dy)
-        by_h1 = input_gradient(1, h1, dy, dg1, du1, G, U)
-        dg0, du0 = hidden(0, False, x, by_h1, G, U, Dn)
-        zero = gradients(0, a0, hid0, dg0, du0, by_h1)
-        summed = [jnp.stack(pair).astype(F32) for pair in zip(zero, one, strict=True)]
-        new = [adamw(w.astype(F32), m, v, g) for w, m, v, g in zip(weights, m, v, summed, strict=True)]
+        *one, by_h1 = gradients(1, a1, hid1, dy, h1, G, U, Dn, dg1, du1)
+        zero = gradients(0, a0, hid0, by_h1, x, G, U, Dn)
+        summed = [jnp.stack(pair).astype(F32) for pair in zip(zero, one)]
+        new = [adamw(w.astype(F32), m, v, g) for w, m, v, g in zip(weights, m, v, summed)]
         return tuple(one[which] for which in range(3) for one in new)
 
-    states, cut = P(("rep", "r", "s"), None, None), P(None, "s", None)
+    states, cut = P(("rep", "r", "s")), P(None, "s")
     return jax.shard_map(
         step,
         mesh=mesh,
         in_specs=(states, states) + (cut,) * 9,
-        out_specs=(P("rep", "s", None),) * 9,
+        out_specs=(P("rep", "s"),) * 9,
         check_vma=False,
     )

time: 577 us -> 516 us (0.89)
  Pallas kernels: 549 us -> 486 us
    pallas_call x2 -> x1, Pallas kernels: 119 us -> 61.6 us  [hidden(): pl.pallas_call(functools.partial(hidden_kernel, number, want_hid), grid=(...]
    pallas_call x1, Pallas kernels: 130 us -> 113 us  [forward(): pl.pallas_call(forward_kernel, out_shape=(jax.ShapeDtypeStruct((2, 8, LAN...]
    pallas_call x3 -> x2, Pallas kernels: 299 us -> 312 us  [gradients(): pl.pallas_call(functools.partial(gradients_kernel, number), out_shape=[ja...]
where the time goes in v3:
time: 516 us; the launch traced here: 508 us
  Pallas kernels  486 us (94%)
  other arithmetic  16.3 us (3%)
    pallas_call x2, Pallas kernels, gradients(): pl.pallas_call(functools.partial(gradients_kernel, number), out_shape=[ja...  312 us
    pallas_call x1, Pallas kernels, forward(): pl.pallas_call(forward_kernel, out_shape=(jax.ShapeDtypeStruct((2, 8, LAN...  113 us
    pallas_call x1, Pallas kernels, hidden(): pl.pallas_call(functools.partial(hidden_kernel, number, want_hid), grid=(...  61.6 us
    convert_element_type x2, other arithmetic, adamw(): return ((w - 0.02 * step).astype(BF), m, v)  16.3 us

profile of v3, /device:TPU:0, one launch (start us, length us, event | category | flops | bytes accessed | tf_op | source)
XLA Modules:
  0.0 507.7 jit_solution(14542976322369311515)
XLA Ops:
  0.6 113.1 %forward.1 = (bf16[2,8,128,3200]{3,2,1,0:T(8,128)(2,1)}, bf16[2,8,128,3200]{3,2,1,0:T(8,128)(2,1)}, bf16[2,8,400,1024]{3,2,1,0:T(8,128)(2,1)}, bf16[3200,2048]{1...) custom-call(bf16[2048,1024]{1,0:T(8,128)(2,1)} %bitcast.19, bf16[2,128,3200]{2,1,0:T(8,128)(2,1)} %g_hbm.1, ...), custom_call_target="tpu_custom_call" | custom-call | flops 40265318400 | bytes 60000000 | tf_op jit(solution)/shard_map/forward/pallas_call | solution.py:261
  113.7 61.6 %hidden_1.1 = (bf16[3200,2048]{1,0:T(8,128)(2,1)}, bf16[1024,2048]{1,0:T(8,128)(2,1)}, bf16[2048,3200]{1,0:T(8,128)(2,1)}, bf16[2048,3200]{1,0:T(8,128)(2,1)}) custom-call(bf16[2048,1024]{1,0:T(8,128)(2,1)} %get-tuple-element.28.h, bf16[2048,1024]{1,0:T(8,128)(2,1)} %bitcast.17, bf16[2,1024,3200]{2,1,0:T(8,128)(2,1)} %bitcast.21, ...), custom_call_target="tpu_custom_call" | custom-call | flops 40265318400 | bytes 70000000 | tf_op jit(solution)/shard_map/hidden_1/pallas_call | solution.py:345
  175.4 150.8 %gradients_1.1 = (bf16[128,3200]{1,0:T(8,128)(2,1)}, bf16[128,3200]{1,0:T(8,128)(2,1)}, bf16[400,1024]{1,0:T(8,128)(2,1)}, bf16[2048,1024]{1,0:T(8,128)(2,1)}) custom-call(bf16[1024,2048]{1,0:T(8,128)(2,1)} %get-tuple-element.32.aT, bf16[3200,2048]{1,0:T(8,128)(2,1)} %get-tuple-element.33.hidT, bf16[2048,1024]{1,0:T(8,128)(2,1)} %bitcast.18, ...), custom_call_target="tpu_custom_call" | custom-call | flops 67108864000 | bytes 60000000 | tf_op jit(solution)/shard_map/gradients_1/pallas_call | solution.py:831
  326.2 160.7 %gradients_0.1 = (bf16[128,3200]{1,0:T(8,128)(2,1)}, bf16[128,3200]{1,0:T(8,128)(2,1)}, bf16[400,1024]{1,0:T(8,128)(2,1)}) custom-call(bf16[1024,2048]{1,0:T(8,128)(2,1)} %get-tuple-element.26.aT, bf16[3200,2048]{1,0:T(8,128)(2,1)} %get-tuple-element.27.hidT, bf16[2048,1024]{1,0:T(8,128)(2,1)} %get-tuple-element.36.by_y, bf16[2048,1024]{1,0:T(8,128)(2,1)} %bitcast.20, ...), custom_call_target="tpu_custom_call" | custom-call | flops 80530636800 | bytes 60000000 | tf_op jit(solution)/shard_map/gradients_0/pallas_call | solution.py:831
  486.9 0.0 copy-start
  486.9 0.0 copy-start.1
  486.9 0.0 copy-start.2
  486.9 0.0 copy-start.3
  486.9 0.0 copy-start.4
  487.0 0.0 copy-start.5
  487.0 0.0 copy-start.6
  487.0 0.0 copy-start.7
  487.0 7.6 %fusion.10 = (bf16[2,400,1024]{2,1,0:T(8,128)(2,1)}, f32[2,400,1024]{2,1,0:T(8,128)}, f32[2,400,1024]{2,1,0:T(8,128)}) fusion(bf16[2,400,1024]{2,1,0:T(8,128)(2,1)} %d_hbm.1, bf16[1,400,1024]{2,1,0:T(8,128)(2,1)} %bitcast.15, bf16[1,400,1024]{2,1,0:T(8,128)(2,1)} %bitcast.16, f32[2,400,1024]{2,1,0:T(8,128)} %param.21, f32[2,400,1024]{2,1,0:T(8,128)} %param.18), kind=kLoop, calls=%fused_computation.22 | loop fusion | flops 15564800 | bytes 18022400 | tf_op jit(solution)/shard_map/convert_element_type | solution.py:862
  494.6 0.0 copy-done
  494.6 1.0 copy-done.1
  495.6 1.0 copy-done.2
  496.5 0.9 copy-done.3
  497.5 0.4 copy-done.4
  497.9 0.5 copy-done.5
  498.4 0.2 copy-done.6
  498.6 0.2 copy-done.7
  498.8 8.7 %fusion.2 = (bf16[2,128,3200]{2,1,0:T(8,128)(2,1)}, f32[2,128,3200]{2,1,0:T(8,128)}, f32[2,128,3200]{2,1,0:T(8,128)}, bf16[2,128,3200]{2,1,0:T(8,128)(2,1)}, f32...) fusion(bf16[2,128,3200]{2,1,0:T(8,128)(2,1)S(1)} %copy-done.4, bf16[1,128,3200]{2,1,0:T(8,128)(2,1)S(1)} %bitcast.11, ...), kind=kLoop, calls=%fused_computation.14 | loop fusion | flops 31129600 | bytes 36044800 | tf_op jit(solution)/shard_map/convert_element_type | solution.py:862
Async XLA Ops:
  486.9 7.7 %copy-start = (f32[2,128,3200]{2,1,0:T(8,128)S(1)}, f32[2,128,3200]{2,1,0:T(8,128)}, u32[]{:S(2)}) copy-start(f32[2,128,3200]{2,1,0:T(8,128)} %param.19) | copy-start | bytes 9830404
  486.9 8.7 %copy-start.1 = (f32[2,128,3200]{2,1,0:T(8,128)S(1)}, f32[2,128,3200]{2,1,0:T(8,128)}, u32[]{:S(2)}) copy-start(f32[2,128,3200]{2,1,0:T(8,128)} %param.16) | copy-start | bytes 9830404
  486.9 9.6 %copy-start.2 = (f32[2,128,3200]{2,1,0:T(8,128)S(1)}, f32[2,128,3200]{2,1,0:T(8,128)}, u32[]{:S(2)}) copy-start(f32[2,128,3200]{2,1,0:T(8,128)} %param.20) | copy-start | bytes 9830404
  486.9 10.5 %copy-start.3 = (f32[2,128,3200]{2,1,0:T(8,128)S(1)}, f32[2,128,3200]{2,1,0:T(8,128)}, u32[]{:S(2)}) copy-start(f32[2,128,3200]{2,1,0:T(8,128)} %param.17) | copy-start | bytes 9830404
  486.9 11.0 %copy-start.4 = (bf16[2,128,3200]{2,1,0:T(8,128)(2,1)S(1)}, bf16[2,128,3200]{2,1,0:T(8,128)(2,1)}, u32[]{:S(2)}) copy-start(bf16[2,128,3200]{2,1,0:T(8,128)(2,1)} %g_hbm.1) | copy-start | bytes 4915204
  487.0 11.4 %copy-start.5 = (bf16[2,128,3200]{2,1,0:T(8,128)(2,1)S(1)}, bf16[2,128,3200]{2,1,0:T(8,128)(2,1)}, u32[]{:S(2)}) copy-start(bf16[2,128,3200]{2,1,0:T(8,128)(2,1)} %u_hbm.1) | copy-start | bytes 4915204
  487.0 11.6 %copy-start.6 = (bf16[128,3200]{1,0:T(8,128)(2,1)S(1)}, bf16[128,3200]{1,0:T(8,128)(2,1)}, u32[]{:S(2)}) copy-start(bf16[128,3200]{1,0:T(8,128)(2,1)} %get-tuple-element.38) | copy-start | bytes 2457604
  487.0 11.8 %copy-start.7 = (bf16[128,3200]{1,0:T(8,128)(2,1)S(1)}, bf16[128,3200]{1,0:T(8,128)(2,1)}, u32[]{:S(2)}) copy-start(bf16[128,3200]{1,0:T(8,128)(2,1)} %get-tuple-element.40) | copy-start | bytes 2457604
